TPU v7x, 32 devices: a whole 2x2x4 slice. The times are simulated.
32 devices in a mesh: wave: 16 (over z, x, core), lev: 2 (over y).
Axes of the slice: x: 2, y: 2, z: 4, core: 2. Of those that a mesh axis runs over, the one named last changes fastest.
Arguments:
- spin_tendency: bfloat16 [32, 2, 136, 768], P('wave', None, 'lev'), may hold values from -6 to 6
- spreading_source: bfloat16 [32, 2, 136, 768], P('wave', None, 'lev'), may hold values from -6 to 6
- heat_source: bfloat16 [32, 2, 136, 768], P('wave', None, 'lev'), may hold values from -6 to 6
- helmholtz_inverses: bfloat16 [2, 384, 136, 136], P('lev', 'wave'), may hold values from -0.5 to 0.5
- heat_spreading_coupler: bfloat16 [136, 136], replicated, may hold values from -0.5 to 0.5
- smoothing_strengths: float32 [136], replicated, may hold values from 0.5 to 30
- azimuthal_order_list: int32 [32], P('wave'), may hold values from 0 to 767
Outputs:
- vorticity_new: bfloat16 [32, 2, 136, 768], P('wave', None, 'lev')
- divergence_new: bfloat16 [32, 2, 136, 768], P('wave', None, 'lev')
- temperature_new: bfloat16 [32, 2, 136, 768], P('wave', None, 'lev')
All inputs are finite; a program needn't handle non-finite values.
Results may differ from a plain program's by a relative error of at most 0.0075.
Values may be sent and summed in bfloat16 or wider, within the bound.
A program may use at most 64 MiB of HBM per device.

v0:
```python
import functools
import jax
import jax.numpy as jnp
from jax import lax
from jax.experimental import pallas as pl
from jax.experimental.pallas import tpu as pltpu
from jax.sharding import PartitionSpec as P

LANES = 128
MESH = pl.DeviceIdType.MESH
NT = (((1,), (1,)), ((), ()))
TN = (((0,), (0,)), ((), ()))


def damping_table(level_gain, wavenumbers, total_n):
    scaled = (wavenumbers * (wavenumbers + 1)).astype(jnp.float32) / jnp.float32(
        (total_n - 1) * total_n
    )
    return 1.0 / (1.0 + level_gain[:, None] * scaled[None, :] ** 2)


def exchange_by_collectives(spreading_source, helmholtz_inverses, heat_spreading_coupler):
    lev_count = lax.axis_size("lev")
    row_count, part_count, lev_local, total_n = spreading_source.shape
    block_n = total_n // lev_count
    layer_count = lev_local * lev_count
    flat_rows = row_count * part_count
    wave_count = lax.axis_size("wave")
    local_n = block_n // wave_count
    rhs_div = lax.all_to_all(spreading_source, "lev", split_axis=3, concat_axis=2, tiled=True)
    outgoing = rhs_div.reshape(flat_rows, layer_count, wave_count, local_n).transpose(2, 3, 0, 1)
    outgoing = outgoing.reshape(wave_count, local_n, flat_rows * layer_count)
    columns = lax.all_to_all(outgoing, "wave", split_axis=0, concat_axis=0, tiled=True)
    columns = columns.reshape(wave_count, local_n, flat_rows, layer_count)
    solved_columns = jnp.einsum(
        "jkp,wjcp->wjck", helmholtz_inverses[0], columns, preferred_element_type=jnp.float32
    ).astype(jnp.bfloat16)
    solved_columns = solved_columns.reshape(wave_count, local_n, flat_rows * layer_count)
    returned = lax.all_to_all(solved_columns, "wave", split_axis=0, concat_axis=0, tiled=True)
    answer_fields = returned.reshape(block_n, flat_rows, layer_count).transpose(1, 2, 0)
    coupled = jnp.einsum(
        "om,dms->dos", heat_spreading_coupler, answer_fields, preferred_element_type=jnp.float32
    ).astype(jnp.bfloat16)
    both = jnp.stack([answer_fields, coupled])
    both = lax.all_to_all(both, "lev", split_axis=2, concat_axis=3, tiled=True)
    both = both.reshape(2, row_count, part_count, lev_local, total_n)
    spreading_updated, coupled_out = both[0], both[1]
    return spreading_updated, coupled_out


def f32_dot(left, right, dims):
    return lax.dot_general(left, right, dims, preferred_element_type=jnp.float32)


def chunk_rows(flat_rows):
    size = max(1, flat_rows // 4)
    cuts = [0, size, flat_rows - size, flat_rows]
    return [range(lo, hi) for lo, hi in zip(cuts, cuts[1:]) if hi > lo]


def exchange_kernel(wave_count, lev_count, chunks, source, matrices, proj, solved_out, coupled_out, *scratch):
    count = len(chunks)
    halves, gathered, strided, results = scratch[:4]
    outgoing, columns, returning, returned = (
        scratch[4 + k * count:4 + (k + 1) * count] for k in range(4)
    )
    (lev_send, lev_recv, wave_send, wave_recv, back_send, back_recv, last_send, last_recv) = scratch[
        4 + 4 * count:
    ]
    wave, lev = lax.axis_index("wave"), lax.axis_index("lev")
    flat_rows, lev_local, total_n = source.shape
    block_n = total_n // lev_count
    local_n = block_n // wave_count
    groups = local_n // 8
    layer_count = lev_local * lev_count
    extra = layer_count - LANES
    wave_peers = [lax.rem(wave + s, wave_count) for s in sorted(range(1, wave_count), key=lambda s: abs(2 * s - wave_count))]
    lev_peers = [lax.rem(lev + s, lev_count) for s in range(1, lev_count)]

    barrier = pltpu.get_barrier_semaphore()
    for peer in wave_peers:
        pl.semaphore_signal(barrier, inc=1, device_id=(peer, lev), device_id_type=MESH)
    for peer in lev_peers:
        pl.semaphore_signal(barrier, inc=1, device_id=(wave, peer), device_id_type=MESH)
    pl.semaphore_wait(barrier, wave_count + lev_count - 2)

    def block_of(index):
        return pl.ds(pl.multiple_of(index * block_n, LANES), block_n)

    def rows_of(c):
        return pl.ds(chunks[c][0], len(chunks[c]))

    lev_copies = []
    for c in range(count):
        for s, peer in enumerate(lev_peers):
            copy = pltpu.make_async_remote_copy(
                src_ref=source.at[rows_of(c), :, block_of(peer)], dst_ref=halves.at[s, rows_of(c)],
                send_sem=lev_send.at[s, c], recv_sem=lev_recv.at[s, c],
                device_id=(wave, peer), device_id_type=MESH,
            )
            copy.start()
            lev_copies.append(copy)

    def shifted(tile, amount):
        amount = amount % LANES
        return pltpu.roll(tile, amount, 1) if amount else tile

    def placed(row, size):
        wide = proj[row]
        first = wide[:, :LANES].astype(jnp.bfloat16)
        rest = wide[:, LANES:]
        return [
            jnp.concatenate([first, shifted(rest, i * extra).astype(jnp.bfloat16)], axis=1)
            for i in range(size)
        ]

    def pack(mains, rest, step):
        rest = rest.reshape(wave_count, groups, 8, LANES)
        folded = rest[:, 0].reshape(wave_count * 8, LANES)
        for g in range(1, groups):
            folded += shifted(rest[:, g].reshape(wave_count * 8, LANES), g * step)
        pieces = [m.reshape(wave_count, local_n, LANES) for m in mains]
        pieces.append(folded.reshape(wave_count, 8, LANES))
        return jnp.concatenate(pieces, axis=1).astype(jnp.bfloat16)

    def unpack(wire, size):
        step = size * extra
        value = wire[...].astype(jnp.float32)
        mains = [
            value[:, i * local_n:(i + 1) * local_n].reshape(block_n, LANES) for i in range(size)
        ]
        folded = value[:, size * local_n:].reshape(wave_count * 8, LANES)
        rest = [
            shifted(folded, -g * step).reshape(wave_count, 1, 8, LANES) for g in range(groups)
        ]
        return mains, jnp.concatenate(rest, axis=1).reshape(block_n, LANES)

    def exchange(src, dst, send_sems, recv_sems, c):
        copies = []
        for s, peer in enumerate(wave_peers):
            copy = pltpu.make_async_remote_copy(
                src_ref=src[c].at[peer], dst_ref=dst[c].at[wave],
                send_sem=send_sems.at[s, c], recv_sem=recv_sems.at[s, c],
                device_id=(peer, lev), device_id_type=MESH,
            )
            copy.start()
            copies.append(copy)
        dst[c][wave] = src[c][wave]
        return copies

    lane = lax.broadcasted_iota(jnp.int32, (wave_count, LANES), 1)
    out_copies, back_copies, last_copies = [], [], []
    for c, chunk in enumerate(chunks):
        size = len(chunk)
        mine = placed(2 * lev, size)
        sums = [f32_dot(source[r, :, block_of(lev)], mine[i], TN) for i, r in enumerate(chunk)]
        for s in range(lev_count - 1):
            lev_copies[c * (lev_count - 1) + s].wait()
            theirs = placed(2 * lax.rem(lev + lev_count - 1 - s, lev_count), size)
            for i, r in enumerate(chunk):
                sums[i] += f32_dot(halves[s, r], theirs[i], TN)
        rest = sum(m[:, LANES:] for m in sums)
        outgoing[c][...] = pack([m[:, :LANES] for m in sums], rest, size * extra)
        out_copies.append(exchange(outgoing, columns, wave_send, wave_recv, c))

    for c, chunk in enumerate(chunks):
        size = len(chunk)
        for copy in out_copies[c]:
            copy.wait()
        mains, rest = unpack(columns[c], size)
        for i, main in enumerate(mains):
            gathered[i] = main
        gathered[size] = rest

        def solve(j, carry):
            rows = pl.ds(j, wave_count, stride=local_n)
            rest = gathered[size, rows, :]
            parts = []
            for i in range(size):
                both = [gathered[i, rows, :], shifted(rest, -i * extra)]
                parts.append(jnp.concatenate(both, axis=1)[:, :layer_count])
            stacked = jnp.concatenate(parts, axis=0).astype(jnp.bfloat16)
            main = f32_dot(stacked, matrices[j, :LANES, :], NT)
            last = f32_dot(stacked, matrices[j, layer_count - LANES:, :], NT)
            rest = jnp.zeros((wave_count, LANES), jnp.float32)
            for i in range(size):
                part = slice(i * wave_count, (i + 1) * wave_count)
                strided[i, rows, :] = main[part]
                keep = (lane >= i * extra) & (lane < (i + 1) * extra)
                rest = jnp.where(keep, shifted(last[part], (i + 1) * extra), rest)
            strided[size, rows, :] = rest
            return carry

        lax.fori_loop(0, local_n, solve, 0, unroll=8)
        returning[c][...] = pack([strided[i] for i in range(size)], strided[size], size * extra)
        back_copies.append(exchange(returning, returned, back_send, back_recv, c))

    for c, chunk in enumerate(chunks):
        size = len(chunk)
        for copy in back_copies[c]:
            copy.wait()
        mains, rest = unpack(returned[c], size)
        pairs = [jnp.concatenate([main, rest], axis=1).astype(jnp.bfloat16) for main in mains]

        def finish(row):
            return [
                f32_dot(weights, pair, NT).astype(jnp.bfloat16)
                for weights, pair in zip(placed(row, size), pairs)
            ]

        for s, peer in enumerate(lev_peers):
            for field, target in enumerate((solved_out, coupled_out)):
                for r, value in zip(chunk, finish(2 * peer + field)):
                    results[s, field, r] = value
                copy = pltpu.make_async_remote_copy(
                    src_ref=results.at[s, field, rows_of(c)],
                    dst_ref=target.at[rows_of(c), :, block_of(lev)],
                    send_sem=last_send.at[s, field, c], recv_sem=last_recv.at[s, field, c],
                    device_id=(wave, peer), device_id_type=MESH,
                )
                copy.start()
                last_copies.append(copy)
        for field, target in enumerate((solved_out, coupled_out)):
            for r, value in zip(chunk, finish(2 * lev + field)):
                target[r, :, block_of(lev)] = value
    for copy in last_copies:
        copy.wait()


def exchange_by_kernel(spreading_source, helmholtz_inverses, heat_spreading_coupler):
    lev_count, wave_count = lax.axis_size("lev"), lax.axis_size("wave")
    row_count, part_count, lev_local, total_n = spreading_source.shape
    block_n = total_n // lev_count
    local_n = block_n // wave_count
    layer_count = lev_local * lev_count
    flat_rows = row_count * part_count
    chunks = chunk_rows(flat_rows)
    longest = max(len(chunk) for chunk in chunks)
    proj = jnp.stack([jnp.eye(layer_count, dtype=jnp.float32), heat_spreading_coupler.astype(jnp.float32)])
    proj = jnp.pad(proj, ((0, 0), (0, 0), (0, 2 * LANES - layer_count)))
    proj = proj.reshape(2, lev_count, lev_local, 2 * LANES).transpose(1, 0, 2, 3)
    proj = proj.reshape(2 * lev_count, lev_local, 2 * LANES)
    vmem = pl.BlockSpec(memory_space=pltpu.VMEM)
    field = jax.ShapeDtypeStruct((flat_rows, lev_local, total_n), jnp.bfloat16)
    wires = [pltpu.VMEM((wave_count, len(c) * local_n + 8, LANES), jnp.bfloat16) for c in chunks]
    wide = pltpu.VMEM((longest + 1, block_n, LANES), jnp.float32)
    dma = pltpu.SemaphoreType.DMA
    lev_sems, wave_sems = dma((lev_count - 1, len(chunks))), dma((wave_count - 1, len(chunks)))
    last_sems = dma((lev_count - 1, 2, len(chunks)))
    solved, coupled = pl.pallas_call(
        functools.partial(exchange_kernel, wave_count, lev_count, chunks),
        out_shape=(field, field),
        in_specs=[vmem] * 3,
        out_specs=(vmem, vmem),
        scratch_shapes=[
            pltpu.VMEM((lev_count - 1, flat_rows, lev_local, block_n), jnp.bfloat16),
            wide, wide,
            pltpu.VMEM((lev_count - 1, 2, flat_rows, lev_local, block_n), jnp.bfloat16),
            *wires, *wires, *wires, *wires,
            lev_sems, lev_sems, wave_sems, wave_sems, wave_sems, wave_sems, last_sems, last_sems,
        ],
        compiler_params=pltpu.CompilerParams(
            collective_id=0, has_side_effects=True, vmem_limit_bytes=48 * 2**20
        ),
    )(spreading_source.reshape(field.shape), helmholtz_inverses[0], proj)
    shape = spreading_source.shape
    return solved.reshape(shape), coupled.reshape(shape)


def kernel_fits(source_shape, lev_count, wave_count):
    row_count, part_count, lev_local, total_n = source_shape
    block_n = total_n // lev_count
    extra = lev_local * lev_count - LANES
    return (
        lev_count > 1
        and wave_count > 1
        and wave_count % 8 == 0
        and block_n % LANES == 0
        and block_n % (8 * wave_count) == 0
        and extra > 0
        and extra * row_count * part_count * (block_n // (8 * wave_count)) <= LANES
    )


def on_device(
    spin_tendency,
    spreading_source,
    heat_source,
    helmholtz_inverses,
    heat_spreading_coupler,
    smoothing_strengths,
    azimuthal_order_list,
):
    lev_count, wave_count = lax.axis_size("lev"), lax.axis_size("wave")
    lev_index = lax.axis_index("lev")
    lev_local, total_n = spreading_source.shape[2:]
    empty_placeholder = jnp.zeros((), jnp.bfloat16)
    fits = kernel_fits(spreading_source.shape, lev_count, wave_count)
    exchange = exchange_by_kernel if fits else exchange_by_collectives
    spreading_updated, coupled_out = exchange(
        spreading_source, helmholtz_inverses, heat_spreading_coupler
    )
    heat_updated = (heat_source.astype(jnp.float32) - coupled_out.astype(jnp.float32)).astype(
        jnp.bfloat16
    )
    level_gain = lax.dynamic_slice_in_dim(smoothing_strengths, lev_index * lev_local, lev_local)
    damping = damping_table(level_gain, jnp.arange(total_n, dtype=jnp.int32), total_n)
    spin_updated = (spin_tendency.astype(jnp.float32) * damping[None, None]).astype(jnp.bfloat16)
    interior_slice = (
        jnp.arange(total_n, dtype=jnp.int32)[None, :] >= azimuthal_order_list[:, None]
    )[:, None, None, :]
    return (
        jnp.where(interior_slice, spin_updated, empty_placeholder),
        jnp.where(interior_slice, spreading_updated, empty_placeholder),
        jnp.where(interior_slice, heat_updated, empty_placeholder),
    )


def solution(mesh):
    return jax.shard_map(
        on_device,
        mesh=mesh,
        in_specs=(
            P("wave", None, "lev", None),
            P("wave", None, "lev", None),
            P("wave", None, "lev", None),
            P("lev", "wave", None, None),
            P(),
            P(),
            P("wave"),
        ),
        out_specs=(
            P("wave", None, "lev", None),
            P("wave", None, "lev", None),
            P("wave", None, "lev", None),
        ),
        check_vma=False,
    )
```

profile of v0, /device:TPU:0, one launch (start us, length us, event | category | flops | bytes accessed | tf_op | source)
XLA Modules:
  0.0 46.9 jit_solution(660247134182127743)
XLA Ops:
  0.6 0.0 copy-start.1
  0.6 0.8 %dynamic_slice.3 = f32[68]{0:T(128)S(1)} dynamic-slice(f32[136]{0:T(256)} %param.12, s32[]{:T(128)S(6)} %select_n.13), dynamic_slice_sizes={68} | dynamic-slice | bytes 548 | tf_op jit(solution)/shard_map/dynamic_slice | solution.py:306
  1.4 0.7 %iota_compare_fusion.1 = pred[2,768]{1,0:T(4,128)(4,1)S(1)} fusion(s32[2]{0:T(128)} %param.13), kind=kLoop, calls=%fused_computation.12 | loop fusion | flops 1536 | bytes 1544 | tf_op jit(solution)/shard_map/ge | solution.py:310
  2.2 0.9 %bitcast_convert_fusion = f32[1,136,136]{2,1,0:T(8,128)S(1)} fusion(bf16[136,136]{1,0:T(8,128)(2,1)} %param.11), kind=kLoop, calls=%fused_computation.10 | loop fusion | flops 18496 | bytes 110976 | tf_op jit(solution)/shard_map/stack | solution.py:239
  3.1 0.0 copy-start
  3.1 0.1 copy.19
  3.3 0.1 pad.4.clone
  3.4 0.1 add_divide_fusion
  3.5 0.0 copy-done.1
  3.6 0.9 %copy-done = bf16[1,24,136,136]{3,2,1,0:T(8,128)(2,1)S(1)} copy-done((bf16[1,24,136,136]{3,2,1,0:T(8,128)(2,1)S(1)}, bf16[1,24,136,136]{3,2,1,0:T(8,128)(2,1)}, u32[]{:S(2)}) %copy-start) | copy-done | bytes 887832
  4.6 0.0 copy-start.2
  4.6 0.0 copy-start.3
  4.6 40.0 %shard_map.94 = (bf16[4,68,768]{2,1,0:T(8,128)(2,1)S(1)}, bf16[4,68,768]{2,1,0:T(8,128)(2,1)S(1)}) custom-call(bf16[4,68,768]{2,1,0:T(8,128)(2,1)S(1)} %bitcast.12, bf16[24,136,136]{2,1,0:T(8,128)(2,1)S(1)} %bitcast.13, f32[4,68,256]{2,1,0:T(8,128)S(1)} %bitcast.14), custom_call_target="tpu_custom_call" | custom-call | tf_op jit(solution)/shard_map/pallas_call | solution.py:250
  44.5 0.1 convert.3
  44.6 0.0 copy-done.2
  44.6 0.0 copy-done.3
  44.6 2.3 %broadcast_select_fusion = (bf16[2,2,68,768]{3,1,2,0:T(2,128)(2,1)}, bf16[2,2,68,768]{3,1,2,0:T(2,128)(2,1)}, bf16[2,2,68,768]{3,1,2,0:T(2,128)(2,1)}) fusion(pred[2,768]{1,0:T(4,128)(4,1)S(1)} %iota_compare_fusion.1, f32[2,2,68,768]{3,2,1,0:T(8,128)S(1)} %convert.3, bf16[2,2,68,768]{3,1,2,0:T(2,128)(2,1)S(1)} %copy-done.2, ...), kind=kLoop, calls=%fused_computation.3 | loop fusion | flops 1880064 | bytes 3552768 | tf_op jit(solution)/shard_map/jit(_where)/select_n | solution.py:315
  (5 shorter events, 0.1 us)
Async XLA Ops:
  0.6 2.9 %copy-start.1 = (bf16[2,2,68,768]{3,1,2,0:T(2,128)(2,1)S(1)}, bf16[2,2,68,768]{3,1,2,0:T(2,128)(2,1)}, u32[]{:S(2)}) copy-start(bf16[2,2,68,768]{3,1,2,0:T(2,128)(2,1)} %param.8) | copy-start | bytes 1253380
  3.1 1.4 %copy-start = (bf16[1,24,136,136]{3,2,1,0:T(8,128)(2,1)S(1)}, bf16[1,24,136,136]{3,2,1,0:T(8,128)(2,1)}, u32[]{:S(2)}) copy-start(bf16[1,24,136,136]{3,2,1,0:T(8,128)(2,1)} %param.10) | copy-start | bytes 2663428
  4.6 40.0 %copy-start.2 = (bf16[2,2,68,768]{3,1,2,0:T(2,128)(2,1)S(1)}, bf16[2,2,68,768]{3,1,2,0:T(2,128)(2,1)}, u32[]{:S(2)}) copy-start(bf16[2,2,68,768]{3,1,2,0:T(2,128)(2,1)} %param.9) | copy-start | bytes 1253380
  4.6 40.1 %copy-start.3 = (bf16[2,2,68,768]{3,1,2,0:T(2,128)(2,1)S(1)}, bf16[2,2,68,768]{3,1,2,0:T(2,128)(2,1)}, u32[]{:S(2)}) copy-start(bf16[2,2,68,768]{3,1,2,0:T(2,128)(2,1)} %param.7) | copy-start | bytes 1253380
where the time goes:
time: 47.1 us; the launch traced here: 46.9 us
  Pallas kernels  40 us (85%)
  other arithmetic  4.09 us (9%)
  local copies, waits for them, and re-layouts  2.07 us (4%)
  between operations  0.75 us (2%)
    pallas_call x1, Pallas kernels, exchange_by_kernel(): pl.pallas_call(functools.partial(exchange_kernel, wave_count, lev_count,...  40 us
    select_n x1, other arithmetic, on_device(): jnp.where(interior_slice, heat_updated, empty_placeholder)  2.26 us
    unnamed x10, local copies, waits for them, and re-layouts  1.15 us

commit v1 on v0

v1 whole, which is shorter than its diff:
```python
import functools
import jax
import jax.numpy as jnp
from jax import lax
from jax.experimental import pallas as pl
from jax.experimental.pallas import tpu as pltpu
from jax.sharding import PartitionSpec as P

LANES = 128
MESH = pl.DeviceIdType.MESH
NN = (((1,), (0,)), ((), ()))
NT = (((1,), (1,)), ((), ()))


def damping_table(level_gain, wavenumbers, total_n):
    scaled = (wavenumbers * (wavenumbers + 1)).astype(jnp.float32) / jnp.float32(
        (total_n - 1) * total_n
    )
    return 1.0 / (1.0 + level_gain[:, None] * scaled[None, :] ** 2)


def exchange_by_collectives(spreading_source, helmholtz_inverses, heat_spreading_coupler):
    lev_count = lax.axis_size("lev")
    row_count, part_count, lev_local, total_n = spreading_source.shape
    block_n = total_n // lev_count
    layer_count = lev_local * lev_count
    flat_rows = row_count * part_count
    wave_count = lax.axis_size("wave")
    local_n = block_n // wave_count
    rhs_div = lax.all_to_all(spreading_source, "lev", split_axis=3, concat_axis=2, tiled=True)
    outgoing = rhs_div.reshape(flat_rows, layer_count, wave_count, local_n).transpose(2, 3, 0, 1)
    outgoing = outgoing.reshape(wave_count, local_n, flat_rows * layer_count)
    columns = lax.all_to_all(outgoing, "wave", split_axis=0, concat_axis=0, tiled=True)
    columns = columns.reshape(wave_count, local_n, flat_rows, layer_count)
    solved_columns = jnp.einsum(
        "jkp,wjcp->wjck", helmholtz_inverses[0], columns, preferred_element_type=jnp.float32
    ).astype(jnp.bfloat16)
    solved_columns = solved_columns.reshape(wave_count, local_n, flat_rows * layer_count)
    returned = lax.all_to_all(solved_columns, "wave", split_axis=0, concat_axis=0, tiled=True)
    answer_fields = returned.reshape(block_n, flat_rows, layer_count).transpose(1, 2, 0)
    coupled = jnp.einsum(
        "om,dms->dos", heat_spreading_coupler, answer_fields, preferred_element_type=jnp.float32
    ).astype(jnp.bfloat16)
    both = jnp.stack([answer_fields, coupled])
    both = lax.all_to_all(both, "lev", split_axis=2, concat_axis=3, tiled=True)
    both = both.reshape(2, row_count, part_count, lev_local, total_n)
    spreading_updated, coupled_out = both[0], both[1]
    return spreading_updated, coupled_out


def f32_dot(left, right, dims):
    return lax.dot_general(left, right, dims, preferred_element_type=jnp.float32)


def grid_of(shape, axis):
    return lax.broadcasted_iota(jnp.int32, shape, axis)


def ones_where(condition, dtype=jnp.bfloat16):
    return jnp.where(condition, 1.0, 0.0).astype(dtype)


def step_kernel(
    wave_count, lev_count, spin, source, heat, matrices, coupler, strengths, orders,
    vort_out, div_out, temp_out,
    spin_in, source_in, heat_in, mats_in, coupler_in, strengths_in, orders_in,
    first_out, next_out, first_in, next_in, gathered, rest_in, tables, strided, rest_out,
    weights, back_out, back_in, relayed,
    load_sem, fwd_send, fwd_recv, back_send, back_recv, relay_send, relay_recv,
):
    wave, lev = lax.axis_index("wave"), lax.axis_index("lev")
    row_count, lev_local, part_count, total_n = source.shape
    block_n = total_n // lev_count
    local_n = block_n // wave_count
    groups = local_n // 8
    layer_count = lev_local * lev_count
    fields = lev_local * part_count
    half = LANES // part_count
    short = lev_local - half
    extra = layer_count - LANES
    depth = tables.shape[1]
    sources = wave_count * lev_count

    loads = []
    for i, (src, dst) in enumerate(
        ((source, source_in), (matrices, mats_in), (coupler, coupler_in), (strengths, strengths_in),
         (orders, orders_in), (spin, spin_in), (heat, heat_in))
    ):
        copy = pltpu.make_async_copy(src, dst, load_sem.at[i])
        copy.start()
        loads.append(copy)

    order = sorted(range(wave_count), key=lambda s: abs(2 * s - wave_count))
    peers = [(lax.rem(wave + s, wave_count), lax.rem(lev + t, lev_count), s * lev_count + t)
             for s in order for t in range(lev_count) if s or t]
    wave_peers = [(lax.rem(wave + s, wave_count), s) for s in order if s]
    arrivals = [(lax.rem(wave + wave_count - s, wave_count), s) for s in order if s]
    barrier = pltpu.get_barrier_semaphore()
    for w, q, _ in peers:
        pl.semaphore_signal(barrier, inc=1, device_id=(w, q), device_id_type=MESH)

    wide = 2 * LANES
    out_row, in_row = grid_of((wide, fields), 0), grid_of((wide, fields), 1)
    level, part = in_row // part_count, in_row % part_count
    main_spot = lax.rem(part + lev, part_count) * half + level
    eye = ones_where(grid_of((wide, wide), 0) == grid_of((wide, wide), 1))
    loads[0].wait()
    flat = source_in.reshape(row_count, fields, total_n)
    mains, rest = [], None
    for r in range(row_count):
        rest_spot = LANES + (r * part_count + part) * extra + lev * short + level - half
        spot = jnp.where(level < half, main_spot, rest_spot)
        picked = f32_dot(ones_where(out_row == spot), flat[r], NN)
        mains.append(picked[:LANES].astype(jnp.bfloat16))
        rest = picked[LANES:] if rest is None else rest + picked[LANES:]
    mains[0] = jnp.concatenate([mains[0], rest.astype(jnp.bfloat16)], axis=0)
    step = row_count * part_count * extra
    for r in range(row_count):
        turned = jnp.concatenate(
            [f32_dot(eye, mains[r][:, k:k + wide], NT) for k in range(0, total_n, wide)], axis=0
        )
        main = turned[:, :LANES].reshape(sources, local_n, LANES)
        if r:
            next_out[r - 1] = main.astype(jnp.bfloat16)
            continue
        tail = turned[:, LANES:].reshape(sources, groups, 8, LANES)
        folded = tail[:, 0].reshape(sources * 8, LANES)
        for g in range(1, groups):
            folded += pltpu.roll(tail[:, g].reshape(sources * 8, LANES), g * step, 1)
        first_out[...] = jnp.concatenate(
            [main, folded.reshape(sources, 8, LANES)], axis=1
        ).astype(jnp.bfloat16)

    pl.semaphore_wait(barrier, sources - 1)
    mine = lev * wave_count + wave

    def outgoing(r):
        return first_out if r == 0 else next_out.at[r - 1]

    def incoming(r):
        return first_in if r == 0 else next_in.at[r - 1]

    fwd = []
    for r in range(row_count):
        fwd.append([])
        for w, q, i in peers:
            copy = pltpu.make_async_remote_copy(
                src_ref=outgoing(r).at[q * wave_count + w], dst_ref=incoming(r).at[mine],
                send_sem=fwd_send.at[r, i], recv_sem=fwd_recv.at[r, i],
                device_id=(w, q), device_id_type=MESH,
            )
            copy.start()
            fwd[r].append(copy)
    for r in range(row_count):
        incoming(r)[mine] = outgoing(r)[mine]

    loads[1].wait()
    deep, flat_level = grid_of((depth, layer_count), 0), grid_of((depth, layer_count), 1)
    owner, place = flat_level // lev_local, flat_level % lev_local
    spot = jnp.where(place < half, owner * half + place, LANES + owner * short + place - half)
    ordered = ones_where(deep == spot)
    lanes = grid_of((depth, LANES), 1)
    zeros = jnp.zeros((depth, LANES - extra), jnp.float32)

    def prepare(s, carry):
        for g in range(groups):
            j = g * 8 + s
            turned = f32_dot(ordered, mats_in[j], NT)
            last = jnp.concatenate([turned[:, LANES:], zeros], axis=1)
            if g:
                last = pltpu.roll(last, g * part_count * extra, 1)
            tables[j] = jnp.concatenate([turned[:, :LANES], last], axis=1).astype(jnp.bfloat16)
        return carry

    lax.fori_loop(0, 8, prepare, 0)

    loads[2].wait()
    row, col = grid_of((fields, layer_count), 0), grid_of((fields, layer_count), 1)
    chosen = ones_where(col == lev * lev_local + row // part_count)
    coupled_rows = f32_dot(chosen, coupler_in[...], NN)
    tops = jnp.concatenate([chosen.astype(jnp.float32), coupled_rows], axis=0)
    tops_part = lax.rem(grid_of(tops.shape, 0), part_count)
    keeps = [jnp.where(tops_part == c, tops, 0.0) for c in range(part_count)]
    pieces = [k[:, :LANES] for k in keeps] + [k[:, LANES:] for k in keeps]
    pieces.append(jnp.zeros((2 * fields, LANES - part_count * extra), jnp.float32))
    weights[...] = jnp.concatenate(pieces, axis=1).astype(jnp.bfloat16)

    for copy in loads[3:6]:
        copy.wait()
    row, col = grid_of((fields, layer_count), 0), grid_of((fields, layer_count), 1)
    gain = jnp.sum(
        jnp.where(col == lev * lev_local + row // part_count, strengths_in[...], 0.0),
        axis=1, keepdims=True,
    )
    n = grid_of((1, total_n), 1)
    scaled = (n * (n + 1)).astype(jnp.float32) / jnp.float32((total_n - 1) * total_n)
    damping = 1.0 / (1.0 + gain * scaled ** 2)
    spin_flat = spin_in.reshape(row_count, fields, total_n)
    vort_flat = vort_out.reshape(row_count, fields, total_n)
    for r in range(row_count):
        value = (spin_flat[r].astype(jnp.float32) * damping)
        value = jnp.where(n >= orders_in[:, r:r + 1], value, 0.0)
        vort_flat[r] = value.astype(jnp.bfloat16)

    lane = grid_of((wave_count, LANES), 1)
    back = []
    for r in range(row_count):
        for copy in fwd[r]:
            copy.wait_recv()
        for p in range(lev_count):
            part_in = incoming(r)[pl.ds(p * wave_count, wave_count)].astype(jnp.float32)
            gathered[p] = part_in[:, :local_n].reshape(block_n, LANES)
            if r == 0:
                value = part_in[:, local_n:].reshape(wave_count * 8, LANES)
                rest_sum = value if p == 0 else rest_sum + value
        if r == 0:
            rest_in[...] = rest_sum

        def solve(s, carry):
            rest = rest_in[pl.ds(s, wave_count, stride=8), :]
            lasts = None
            for g in range(groups):
                j = g * 8 + s
                rows = pl.ds(j, wave_count, stride=local_n)
                low, high = gathered[0, rows, :], gathered[1, rows, :]
                sides = [jnp.where(lane < half, low, high),
                         pltpu.roll(jnp.where(lane < half, high, low), half, 1)]
                stacked = []
                for c in range(part_count):
                    shift = g * step + (r * part_count + c) * extra
                    moved = pltpu.roll(rest, LANES - shift, 1) if shift else rest
                    stacked.append(jnp.concatenate([sides[c], moved], axis=1)[:, :depth])
                stacked = jnp.concatenate(stacked, axis=0).astype(jnp.bfloat16)
                result = f32_dot(stacked, tables[j], NN)
                for c in range(part_count):
                    strided[c, rows, :] = result[c * wave_count:(c + 1) * wave_count, :LANES]
                last = result[:, LANES:]
                lasts = last if lasts is None else lasts + last
            total = lasts[:wave_count]
            for c in range(1, part_count):
                total += pltpu.roll(lasts[c * wave_count:(c + 1) * wave_count], c * extra, 1)
            rest_out[pl.ds(s, wave_count, stride=8), :] = total
            return carry

        lax.fori_loop(0, 8, solve, 0, unroll=2)
        pieces = [strided[c].reshape(wave_count, local_n, LANES) for c in range(part_count)]
        pieces.append(rest_out[...].reshape(wave_count, 8, LANES))
        back_out[r] = jnp.concatenate(pieces, axis=1).astype(jnp.bfloat16)
        back.append([])
        for w, s in wave_peers:
            copy = pltpu.make_async_remote_copy(
                src_ref=back_out.at[r, w], dst_ref=back_in.at[r, wave],
                send_sem=back_send.at[r, s], recv_sem=back_recv.at[r, s],
                device_id=(w, lev), device_id_type=MESH,
            )
            copy.start()
            back[r].append(copy)
        back_in[r, wave] = back_out[r, wave]

    relays = [[] for _ in range(row_count)]
    other = lax.rem(lev + 1, lev_count)

    def relay(r, spot, index):
        copy = pltpu.make_async_remote_copy(
            src_ref=back_in.at[r, spot], dst_ref=relayed.at[r, spot],
            send_sem=relay_send.at[r, index], recv_sem=relay_recv.at[r, index],
            device_id=(wave, other), device_id_type=MESH,
        )
        copy.start()
        relays[r].append(copy)

    heat_flat = heat_in.reshape(row_count, fields, total_n)
    div_flat = div_out.reshape(row_count, fields, total_n)
    temp_flat = temp_out.reshape(row_count, fields, total_n)

    def finish(r, wire, block):
        value = wire[r].astype(jnp.float32)
        sides = [value[:, c * local_n:(c + 1) * local_n].reshape(block_n, LANES)
                 for c in range(part_count)]
        folded = value[:, part_count * local_n:].reshape(wave_count * 8, LANES)
        turn = part_count * extra
        rest = [(pltpu.roll(folded, LANES - g * turn, 1) if g else folded)
                .reshape(wave_count, 1, 8, LANES) for g in range(groups)]
        sides.append(jnp.concatenate(rest, axis=1).reshape(block_n, LANES))
        packed = jnp.concatenate(sides, axis=1).astype(jnp.bfloat16)
        result = f32_dot(weights[...], packed, NT)
        spots = pl.ds(pl.multiple_of(block * block_n, LANES), block_n)
        inside = block * block_n + grid_of((1, block_n), 1) >= orders_in[:, r:r + 1]
        div_flat[r, :, spots] = jnp.where(inside, result[:fields], 0.0).astype(jnp.bfloat16)
        coupled = result[fields:].astype(jnp.bfloat16).astype(jnp.float32)
        warmed = heat_flat[r, :, spots].astype(jnp.float32) - coupled
        temp_flat[r, :, spots] = jnp.where(inside, warmed, 0.0).astype(jnp.bfloat16)

    loads[6].wait()
    for r in range(row_count):
        relay(r, wave, 0)
        for (w, s), copy in zip(arrivals, back[r]):
            copy.wait_recv()
            relay(r, w, s)
        finish(r, back_in, lev)
        if r:
            for copy in relays[r - 1]:
                copy.wait_recv()
            finish(r - 1, relayed, other)
    for copy in relays[-1]:
        copy.wait_recv()
    finish(row_count - 1, relayed, other)
    for group in (*fwd, *back, *relays):
        for copy in group:
            copy.wait_send()


def by_kernel(spin, source, heat, matrices, coupler, strengths, orders):
    lev_count, wave_count = lax.axis_size("lev"), lax.axis_size("wave")
    row_count, part_count, lev_local, total_n = source.shape
    block_n = total_n // lev_count
    local_n = block_n // wave_count
    layer_count = lev_local * lev_count
    fields = lev_local * part_count
    sources = wave_count * lev_count
    depth = -(-layer_count // 16) * 16
    anywhere, vmem = pl.BlockSpec(memory_space=pl.ANY), pl.BlockSpec(memory_space=pltpu.VMEM)
    shape = (row_count, lev_local, part_count, total_n)
    bf16, f32 = jnp.bfloat16, jnp.float32
    field = jax.ShapeDtypeStruct(shape, bf16)
    dma = pltpu.SemaphoreType.DMA
    back_rows = part_count * local_n + 8
    wire = pltpu.VMEM((row_count, wave_count, back_rows, LANES), bf16)
    outs = pl.pallas_call(
        functools.partial(step_kernel, wave_count, lev_count),
        out_shape=(field,) * 3,
        in_specs=[anywhere] * 7,
        out_specs=(vmem,) * 3,
        scratch_shapes=[
            pltpu.VMEM(shape, bf16), pltpu.VMEM(shape, bf16), pltpu.VMEM(shape, bf16),
            pltpu.VMEM(matrices.shape[1:], bf16), pltpu.VMEM(coupler.shape, bf16),
            pltpu.VMEM((1, layer_count), f32), pltpu.VMEM((1, row_count), jnp.int32),
            pltpu.VMEM((sources, local_n + 8, LANES), bf16),
            pltpu.VMEM((row_count - 1, sources, local_n, LANES), bf16),
            pltpu.VMEM((sources, local_n + 8, LANES), bf16),
            pltpu.VMEM((row_count - 1, sources, local_n, LANES), bf16),
            pltpu.VMEM((lev_count, block_n, LANES), f32),
            pltpu.VMEM((wave_count * 8, LANES), f32),
            pltpu.VMEM((local_n, depth, 2 * LANES), bf16),
            pltpu.VMEM((part_count, block_n, LANES), f32),
            pltpu.VMEM((wave_count * 8, LANES), f32),
            pltpu.VMEM((2 * fields, 3 * LANES), bf16),
            wire, wire, wire,
            dma((7,)),
            dma((row_count, sources)), dma((row_count, sources)),
            dma((row_count, wave_count)), dma((row_count, wave_count)),
            dma((row_count, wave_count)), dma((row_count, wave_count)),
        ],
        compiler_params=pltpu.CompilerParams(
            collective_id=0, has_side_effects=True, vmem_limit_bytes=48 * 2**20
        ),
    )(
        spin.transpose(0, 2, 1, 3), source.transpose(0, 2, 1, 3), heat.transpose(0, 2, 1, 3),
        matrices[0], coupler, strengths.reshape(1, layer_count), orders.reshape(1, row_count),
    )
    return tuple(out.transpose(0, 2, 1, 3) for out in outs)


def kernel_fits(source_shape, lev_count, wave_count):
    row_count, part_count, lev_local, total_n = source_shape
    block_n = total_n // lev_count
    extra = lev_local * lev_count - LANES
    return (
        lev_count == 2
        and part_count == 2
        and row_count > 1
        and wave_count > 1
        and wave_count % 8 == 0
        and block_n % LANES == 0
        and total_n % (2 * LANES) == 0
        and block_n % (8 * wave_count) == 0
        and extra > 0
        and extra * row_count * part_count * (block_n // (8 * wave_count)) <= LANES
    )


def on_device(
    spin_tendency,
    spreading_source,
    heat_source,
    helmholtz_inverses,
    heat_spreading_coupler,
    smoothing_strengths,
    azimuthal_order_list,
):
    lev_count, wave_count = lax.axis_size("lev"), lax.axis_size("wave")
    lev_index = lax.axis_index("lev")
    lev_local, total_n = spreading_source.shape[2:]
    empty_placeholder = jnp.zeros((), jnp.bfloat16)
    if kernel_fits(spreading_source.shape, lev_count, wave_count):
        return by_kernel(
            spin_tendency, spreading_source, heat_source, helmholtz_inverses,
            heat_spreading_coupler, smoothing_strengths, azimuthal_order_list,
        )
    spreading_updated, coupled_out = exchange_by_collectives(
        spreading_source, helmholtz_inverses, heat_spreading_coupler
    )
    heat_updated = (heat_source.astype(jnp.float32) - coupled_out.astype(jnp.float32)).astype(
        jnp.bfloat16
    )
    level_gain = lax.dynamic_slice_in_dim(smoothing_strengths, lev_index * lev_local, lev_local)
    damping = damping_table(level_gain, jnp.arange(total_n, dtype=jnp.int32), total_n)
    spin_updated = (spin_tendency.astype(jnp.float32) * damping[None, None]).astype(jnp.bfloat16)
    interior_slice = (
        jnp.arange(total_n, dtype=jnp.int32)[None, :] >= azimuthal_order_list[:, None]
    )[:, None, None, :]
    return (
        jnp.where(interior_slice, spin_updated, empty_placeholder),
        jnp.where(interior_slice, spreading_updated, empty_placeholder),
        jnp.where(interior_slice, heat_updated, empty_placeholder),
    )


def solution(mesh):
    return jax.shard_map(
        on_device,
        mesh=mesh,
        in_specs=(
            P("wave", None, "lev", None),
            P("wave", None, "lev", None),
            P("wave", None, "lev", None),
            P("lev", "wave", None, None),
            P(),
            P(),
            P("wave"),
        ),
        out_specs=(
            P("wave", None, "lev", None),
            P("wave", None, "lev", None),
            P("wave", None, "lev", None),
        ),
        check_vma=False,
    )
```

time: 47.1 us -> 47.7 us (1.013)
  local copies, waits for them, and re-layouts: 2.07 us -> 8.93 us
  other arithmetic: 4.09 us -> 0 us
  Pallas kernels: 40 us -> 37.7 us
    unnamed x10 -> x17, local copies, waits for them, and re-layouts: 1.15 us -> 8.93 us
    select_n x1 -> x0, other arithmetic: 2.26 us -> none  [on_device(): jnp.where(interior_slice, heat_updated, empty_placeholder)]
    pallas_call x1, Pallas kernels: 40 us -> 37.7 us  [by_kernel(): pl.pallas_call(functools.partial(step_kernel, wave_count, lev_count), out...]
    another operation x2 -> x0, other arithmetic: 0.92 us -> none  [exchange_by_kernel(): jnp.stack([jnp.eye(layer_count, dtype=jnp.float32), heat_spreading_couple...]
    dynamic_slice x1 -> x0, local copies, waits for them, and re-layouts: 0.81 us -> none  [on_device(): lax.dynamic_slice_in_dim(smoothing_strengths, lev_index * lev_local, lev_...]
    ge x1 -> x0, other arithmetic: 0.73 us -> none  [on_device(): jnp.arange(total_n, dtype=jnp.int32)[None, :]]
where the time goes in v1:
time: 47.7 us; the launch traced here: 47.3 us
  Pallas kernels  37.7 us (79%)
  local copies, waits for them, and re-layouts  8.93 us (19%)
  between operations  0.66 us (1%)
    pallas_call x1, Pallas kernels, by_kernel(): pl.pallas_call(functools.partial(step_kernel, wave_count, lev_count), out...  37.7 us
    unnamed x17, local copies, waits for them, and re-layouts  8.93 us

profile of v1, /device:TPU:0, one launch (start us, length us, event | category | flops | bytes accessed | tf_op | source)
XLA Modules:
  0.0 47.3 jit_solution(15725806975577505255)
XLA Ops:
  0.6 0.0 copy-start
  0.6 1.4 %copy-done = bf16[1,24,136,136]{3,2,1,0:T(8,128)(2,1)S(1)} copy-done((bf16[1,24,136,136]{3,2,1,0:T(8,128)(2,1)S(1)}, bf16[1,24,136,136]{3,2,1,0:T(8,128)(2,1)}, u32[]{:S(2)}) %copy-start) | copy-done | bytes 887832
  2.1 0.0 copy-start.1
  2.1 1.0 %copy-done.1 = bf16[2,2,68,768]{3,1,2,0:T(2,128)(2,1)S(1)} copy-done((bf16[2,2,68,768]{3,1,2,0:T(2,128)(2,1)S(1)}, bf16[2,2,68,768]{3,1,2,0:T(2,128)(2,1)}, u32[]{:S(2)}) %copy-start.1) | copy-done | bytes 417816
  3.1 0.0 copy-start.2
  3.1 1.0 %copy-done.2 = bf16[2,2,68,768]{3,1,2,0:T(2,128)(2,1)S(1)} copy-done((bf16[2,2,68,768]{3,1,2,0:T(2,128)(2,1)S(1)}, bf16[2,2,68,768]{3,1,2,0:T(2,128)(2,1)}, u32[]{:S(2)}) %copy-start.2) | copy-done | bytes 417816
  4.1 0.0 copy-start.3
  4.1 1.0 %copy-done.3 = bf16[2,2,68,768]{3,1,2,0:T(2,128)(2,1)S(1)} copy-done((bf16[2,2,68,768]{3,1,2,0:T(2,128)(2,1)S(1)}, bf16[2,2,68,768]{3,1,2,0:T(2,128)(2,1)}, u32[]{:S(2)}) %copy-start.3) | copy-done | bytes 417816
  5.1 0.0 copy-start.4
  5.1 0.9 %copy-done.4 = bf16[136,136]{1,0:T(8,128)(2,1)S(1)} copy-done((bf16[136,136]{1,0:T(8,128)(2,1)S(1)}, bf16[136,136]{1,0:T(8,128)(2,1)}, u32[]{:S(2)}) %copy-start.4) | copy-done | bytes 37016
  6.0 0.0 copy-start.5
  6.0 0.7 %copy-done.5 = f32[136]{0:T(256)S(1)} copy-done((f32[136]{0:T(256)S(1)}, f32[136]{0:T(256)}, u32[]{:S(2)}) %copy-start.5) | copy-done | bytes 568
  6.7 0.0 copy-start.6
  6.7 0.7 %copy-done.6 = s32[2]{0:T(128)S(1)} copy-done((s32[2]{0:T(128)S(1)}, s32[2]{0:T(128)}, u32[]{:S(2)}) %copy-start.6) | copy-done | bytes 32
  7.3 37.7 %shard_map.94 = (bf16[2,68,2,768]{3,2,1,0:T(2,128)(2,1)S(1)}, bf16[2,68,2,768]{3,2,1,0:T(2,128)(2,1)S(1)}, bf16[2,68,2,768]{3,2,1,0:T(2,128)(2,1)S(1)}) custom-call(bf16[2,68,2,768]{3,2,1,0:T(2,128)(2,1)S(1)} %bitcast.10, bf16[2,68,2,768]{3,2,1,0:T(2,128)(2,1)S(1)} %bitcast.11, bf16[2,68,2,768]{3,2,1,0:T(2,128)(2,1)S(1)} %bitcast.12, ...), custom_call_target="tpu_custom_call" | custom-call | tf_op jit(solution)/shard_map/pallas_call | solution.py:329
  45.1 0.8 %copy.13 = bf16[2,2,68,768]{3,1,2,0:T(2,128)(2,1)} copy(bf16[2,2,68,768]{3,1,2,0:T(2,128)(2,1)S(1)} %bitcast.15) | data formatting | bytes 835584
  45.8 0.8 %copy.14 = bf16[2,2,68,768]{3,1,2,0:T(2,128)(2,1)} copy(bf16[2,2,68,768]{3,1,2,0:T(2,128)(2,1)S(1)} %bitcast.14) | data formatting | bytes 835584
  46.6 0.8 %copy.15 = bf16[2,2,68,768]{3,1,2,0:T(2,128)(2,1)} copy(bf16[2,2,68,768]{3,1,2,0:T(2,128)(2,1)S(1)} %bitcast.13) | data formatting | bytes 835584
Async XLA Ops:
  0.6 1.4 %copy-start = (bf16[1,24,136,136]{3,2,1,0:T(8,128)(2,1)S(1)}, bf16[1,24,136,136]{3,2,1,0:T(8,128)(2,1)}, u32[]{:S(2)}) copy-start(bf16[1,24,136,136]{3,2,1,0:T(8,128)(2,1)} %param.10) | copy-start | bytes 2663428
  2.1 1.0 %copy-start.1 = (bf16[2,2,68,768]{3,1,2,0:T(2,128)(2,1)S(1)}, bf16[2,2,68,768]{3,1,2,0:T(2,128)(2,1)}, u32[]{:S(2)}) copy-start(bf16[2,2,68,768]{3,1,2,0:T(2,128)(2,1)} %param.7) | copy-start | bytes 1253380
  3.1 1.0 %copy-start.2 = (bf16[2,2,68,768]{3,1,2,0:T(2,128)(2,1)S(1)}, bf16[2,2,68,768]{3,1,2,0:T(2,128)(2,1)}, u32[]{:S(2)}) copy-start(bf16[2,2,68,768]{3,1,2,0:T(2,128)(2,1)} %param.8) | copy-start | bytes 1253380
  4.1 1.0 %copy-start.3 = (bf16[2,2,68,768]{3,1,2,0:T(2,128)(2,1)S(1)}, bf16[2,2,68,768]{3,1,2,0:T(2,128)(2,1)}, u32[]{:S(2)}) copy-start(bf16[2,2,68,768]{3,1,2,0:T(2,128)(2,1)} %param.9) | copy-start | bytes 1253380
  5.1 0.9 %copy-start.4 = (bf16[136,136]{1,0:T(8,128)(2,1)S(1)}, bf16[136,136]{1,0:T(8,128)(2,1)}, u32[]{:S(2)}) copy-start(bf16[136,136]{1,0:T(8,128)(2,1)} %coupler.1) | copy-start | bytes 110980
  6.0 0.7 %copy-start.5 = (f32[136]{0:T(256)S(1)}, f32[136]{0:T(256)}, u32[]{:S(2)}) copy-start(f32[136]{0:T(256)} %param.12) | copy-start | bytes 1636
  6.7 0.7 %copy-start.6 = (s32[2]{0:T(128)S(1)}, s32[2]{0:T(128)}, u32[]{:S(2)}) copy-start(s32[2]{0:T(128)} %param.13) | copy-start | bytes 28

commit v2 on v1

--- a/solution.py
+++ b/solution.py
@@ -310,6 +310,17 @@
             copy.wait_send()
 
 
+def store_kernel(*refs):
+    count = (len(refs) - 1) // 2
+    copies = [
+        pltpu.make_async_copy(refs[i], refs[count + i], refs[-1].at[i]) for i in range(count)
+    ]
+    for copy in copies:
+        copy.start()
+    for copy in copies:
+        copy.wait()
+
+
 def by_kernel(spin, source, heat, matrices, coupler, strengths, orders):
     lev_count, wave_count = lax.axis_size("lev"), lax.axis_size("wave")
     row_count, part_count, lev_local, total_n = source.shape
@@ -319,7 +330,7 @@
     fields = lev_local * part_count
     sources = wave_count * lev_count
     depth = -(-layer_count // 16) * 16
-    anywhere, vmem = pl.BlockSpec(memory_space=pl.ANY), pl.BlockSpec(memory_space=pltpu.VMEM)
+    anywhere, vmem = pl.BlockSpec(memory_space=pltpu.HBM), pl.BlockSpec(memory_space=pltpu.VMEM)
     shape = (row_count, lev_local, part_count, total_n)
     bf16, f32 = jnp.bfloat16, jnp.float32
     field = jax.ShapeDtypeStruct(shape, bf16)
@@ -355,9 +366,19 @@
             collective_id=0, has_side_effects=True, vmem_limit_bytes=48 * 2**20
         ),
     )(
-        spin.transpose(0, 2, 1, 3), source.transpose(0, 2, 1, 3), heat.transpose(0, 2, 1, 3),
-        matrices[0], coupler, strengths.reshape(1, layer_count), orders.reshape(1, row_count),
-    )
+        *(
+            pltpu.with_memory_space_constraint(value, pltpu.HBM)
+            for value in (
+                spin.transpose(0, 2, 1, 3), source.transpose(0, 2, 1, 3), heat.transpose(0, 2, 1, 3),
+                matrices[0], coupler, strengths.reshape(1, layer_count), orders.reshape(1, row_count),
+            )
+        )
+    )
+    outs = pl.pallas_call(
+        store_kernel, out_shape=(field,) * 3, in_specs=[vmem] * 3, out_specs=(anywhere,) * 3,
+        scratch_shapes=[dma((3,))],
+        compiler_params=pltpu.CompilerParams(vmem_limit_bytes=4 * 2**20),
+    )(*outs)
     return tuple(out.transpose(0, 2, 1, 3) for out in outs)
 
 

time: 47.7 us -> 38.3 us (0.80)
  local copies, waits for them, and re-layouts: 8.93 us -> 0 us
    unnamed x17 -> x0, local copies, waits for them, and re-layouts: 8.93 us -> none
    pallas_call x1, Pallas kernels: 37.7 us -> 36.4 us  [by_kernel(): pl.pallas_call(functools.partial(step_kernel, wave_count, lev_count), out...]
    pallas_call x0 -> x1, Pallas kernels: none -> 1.06 us  [by_kernel(): pl.pallas_call(store_kernel, out_shape=(field,) * 3, in_specs=[vmem] * 3,...]
where the time goes in v2:
time: 38.3 us; the launch traced here: 38.1 us
  Pallas kernels  37.5 us (98%)
  between operations  0.64 us (2%)
    pallas_call x1, Pallas kernels, by_kernel(): pl.pallas_call(functools.partial(step_kernel, wave_count, lev_count), out...  36.4 us
    pallas_call x1, Pallas kernels, by_kernel(): pl.pallas_call(store_kernel, out_shape=(field,) * 3, in_specs=[vmem] * 3,...  1.06 us

profile of v2, /device:TPU:0, one launch (start us, length us, event | category | flops | bytes accessed | tf_op | source)
XLA Modules:
  0.0 38.1 jit_solution(5829904414218189189)
XLA Ops:
  0.6 36.4 %shard_map.94 = (bf16[2,68,2,768]{3,2,1,0:T(2,128)(2,1)S(1)}, bf16[2,68,2,768]{3,2,1,0:T(2,128)(2,1)S(1)}, bf16[2,68,2,768]{3,2,1,0:T(2,128)(2,1)S(1)}) custom-call(bf16[2,68,2,768]{3,2,1,0:T(2,128)(2,1)} %bitcast.10, bf16[2,68,2,768]{3,2,1,0:T(2,128)(2,1)} %bitcast.11, bf16[2,68,2,768]{3,2,1,0:T(2,128)(2,1)} %bitcast.12, bf16[24,136,136]{2,1,0:T(8,128)(2,1)} %bitcast.9, ...), custom_call_target="tpu_custom_call" | custom-call | tf_op jit(solution)/shard_map/pallas_call | solution.py:340
  37.1 1.1 %shard_map.95 = (bf16[2,68,2,768]{3,2,1,0:T(2,128)(2,1)}, bf16[2,68,2,768]{3,2,1,0:T(2,128)(2,1)}, bf16[2,68,2,768]{3,2,1,0:T(2,128)(2,1)}) custom-call(bf16[2,68,2,768]{3,2,1,0:T(2,128)(2,1)S(1)} %get-tuple-element.9.refs_0_, bf16[2,68,2,768]{3,2,1,0:T(2,128)(2,1)S(1)} %get-tuple-element.10.refs_1_, bf16[2,68,2,768]{3,2,1,0:T(2,128)(2,1)S(1)} %get-tuple-element.11.refs_2_), custom_call_target="tpu_custom_call" | custom-call | tf_op jit(solution)/shard_map/pallas_call | solution.py:377

commit v3 on v2

--- a/solution.py
+++ b/solution.py
@@ -60,6 +60,15 @@
     return jnp.where(condition, 1.0, 0.0).astype(dtype)
 
 
+def flipped(value, mask):
+    out, bit = value, 1
+    while bit <= mask:
+        if mask & bit:
+            out = out + bit * (1 - 2 * lax.rem(lax.div(value, bit), 2))
+        bit *= 2
+    return out
+
+
 def step_kernel(
     wave_count, lev_count, spin, source, heat, matrices, coupler, strengths, orders,
     vort_out, div_out, temp_out,
@@ -80,101 +89,130 @@
     extra = layer_count - LANES
     depth = tables.shape[1]
     sources = wave_count * lev_count
+    wide = 2 * LANES
+    cells = [(h, g) for h in range(2) for g in range(groups)]
+    fwd_step = row_count * part_count * short
+    back_step = part_count * extra
+    rest_step = row_count * part_count * extra
 
     loads = []
+    small = [(matrices, mats_in), (coupler, coupler_in), (strengths, strengths_in),
+             (orders, orders_in), (spin, spin_in), (heat, heat_in)]
     for i, (src, dst) in enumerate(
-        ((source, source_in), (matrices, mats_in), (coupler, coupler_in), (strengths, strengths_in),
-         (orders, orders_in), (spin, spin_in), (heat, heat_in))
+        [(source.at[r], source_in.at[r]) for r in range(row_count)] + small
     ):
         copy = pltpu.make_async_copy(src, dst, load_sem.at[i])
         copy.start()
         loads.append(copy)
-
-    order = sorted(range(wave_count), key=lambda s: abs(2 * s - wave_count))
-    peers = [(lax.rem(wave + s, wave_count), lax.rem(lev + t, lev_count), s * lev_count + t)
-             for s in order for t in range(lev_count) if s or t]
-    wave_peers = [(lax.rem(wave + s, wave_count), s) for s in order if s]
-    arrivals = [(lax.rem(wave + wave_count - s, wave_count), s) for s in order if s]
+    source_loads, loads = loads[:row_count], loads[row_count:]
+
+    peer = [flipped(wave, mask) for mask in range(wave_count)]
+    other = lax.rem(lev + 1, lev_count)
+    far_first = range(wave_count - 1, -1, -1)
     barrier = pltpu.get_barrier_semaphore()
-    for w, q, _ in peers:
-        pl.semaphore_signal(barrier, inc=1, device_id=(w, q), device_id_type=MESH)
-
-    wide = 2 * LANES
+    for mask in far_first:
+        for t, q in enumerate((lev, other)):
+            if mask or t:
+                pl.semaphore_signal(
+                    barrier, inc=1, device_id=(peer[mask], q), device_id_type=MESH
+                )
+
     out_row, in_row = grid_of((wide, fields), 0), grid_of((wide, fields), 1)
     level, part = in_row // part_count, in_row % part_count
     main_spot = lax.rem(part + lev, part_count) * half + level
+    main_pick = ones_where(
+        (out_row == main_spot)[:LANES] & (level < half)[:LANES]
+    )
+    rest_picks = [
+        ones_where(
+            (out_row == (r * part_count + part) * short + level - half)[:LANES]
+            & (level >= half)[:LANES]
+        )
+        for r in range(row_count)
+    ]
     eye = ones_where(grid_of((wide, wide), 0) == grid_of((wide, wide), 1))
+    flat = source_in.reshape(row_count, fields, total_n)
+    mine = lev * wave_count + wave
+
+    def turn(rows):
+        return jnp.concatenate(
+            [f32_dot(eye, rows[:, k:k + wide], NT) for k in range(0, total_n, wide)], axis=0
+        )
+
+    def by_rows(ref):
+        return ref.reshape(*ref.shape[:-3], ref.shape[-3] * 2, LANES)
+
+    outgoing, incoming = [first_out, next_out], [first_in, next_in]
+    fwd = []
+
+    def send(r):
+        fwd.append([])
+        for mask in far_first:
+            for t, q in enumerate((lev, other)):
+                if not (mask or t):
+                    continue
+                copy = pltpu.make_async_remote_copy(
+                    src_ref=outgoing[r].at[q * wave_count + peer[mask]],
+                    dst_ref=incoming[r].at[mine],
+                    send_sem=fwd_send.at[r, mask, t], recv_sem=fwd_recv.at[r, mask, t],
+                    device_id=(peer[mask], q), device_id_type=MESH,
+                )
+                copy.start()
+                fwd[r].append(copy)
+        incoming[r][mine] = outgoing[r][mine]
+
+    for copy in source_loads:
+        copy.wait()
+    main = f32_dot(main_pick, flat[0], NN)
+    rest = f32_dot(rest_picks[0], flat[0], NN)
+    for r in range(1, row_count):
+        rest += f32_dot(rest_picks[r], flat[r], NN)
+    turned = turn(jnp.concatenate([main, rest], axis=0).astype(jnp.bfloat16))
+    tail = turned[:, LANES:].reshape(sources, groups, 8, LANES)
+    folded = tail[:, 0].reshape(sources * 8, LANES)
+    for g in range(1, groups):
+        folded += pltpu.roll(tail[:, g].reshape(sources * 8, LANES), g * fwd_step, 1)
+    swung = pltpu.roll(folded, half, 1).reshape(sources, 8, LANES)
+    folded = folded.reshape(sources, 8, LANES)[:, :4] + swung[:, 4:]
+    by_rows(first_out)[:, :local_n] = (
+        turned[:, :LANES].reshape(sources, local_n, LANES).astype(jnp.bfloat16)
+    )
+    by_rows(first_out)[:, local_n:] = folded.astype(jnp.bfloat16)
+    pl.semaphore_wait(barrier, sources - 1)
+    send(0)
+    for r in range(1, row_count):
+        turned = turn(f32_dot(main_pick, flat[r], NN).astype(jnp.bfloat16))
+        by_rows(next_out)[...] = turned.reshape(sources, local_n, LANES).astype(jnp.bfloat16)
+        send(r)
+
     loads[0].wait()
-    flat = source_in.reshape(row_count, fields, total_n)
-    mains, rest = [], None
-    for r in range(row_count):
-        rest_spot = LANES + (r * part_count + part) * extra + lev * short + level - half
-        spot = jnp.where(level < half, main_spot, rest_spot)
-        picked = f32_dot(ones_where(out_row == spot), flat[r], NN)
-        mains.append(picked[:LANES].astype(jnp.bfloat16))
-        rest = picked[LANES:] if rest is None else rest + picked[LANES:]
-    mains[0] = jnp.concatenate([mains[0], rest.astype(jnp.bfloat16)], axis=0)
-    step = row_count * part_count * extra
-    for r in range(row_count):
-        turned = jnp.concatenate(
-            [f32_dot(eye, mains[r][:, k:k + wide], NT) for k in range(0, total_n, wide)], axis=0
-        )
-        main = turned[:, :LANES].reshape(sources, local_n, LANES)
-        if r:
-            next_out[r - 1] = main.astype(jnp.bfloat16)
-            continue
-        tail = turned[:, LANES:].reshape(sources, groups, 8, LANES)
-        folded = tail[:, 0].reshape(sources * 8, LANES)
-        for g in range(1, groups):
-            folded += pltpu.roll(tail[:, g].reshape(sources * 8, LANES), g * step, 1)
-        first_out[...] = jnp.concatenate(
-            [main, folded.reshape(sources, 8, LANES)], axis=1
-        ).astype(jnp.bfloat16)
-
-    pl.semaphore_wait(barrier, sources - 1)
-    mine = lev * wave_count + wave
-
-    def outgoing(r):
-        return first_out if r == 0 else next_out.at[r - 1]
-
-    def incoming(r):
-        return first_in if r == 0 else next_in.at[r - 1]
-
-    fwd = []
-    for r in range(row_count):
-        fwd.append([])
-        for w, q, i in peers:
-            copy = pltpu.make_async_remote_copy(
-                src_ref=outgoing(r).at[q * wave_count + w], dst_ref=incoming(r).at[mine],
-                send_sem=fwd_send.at[r, i], recv_sem=fwd_recv.at[r, i],
-                device_id=(w, q), device_id_type=MESH,
-            )
-            copy.start()
-            fwd[r].append(copy)
-    for r in range(row_count):
-        incoming(r)[mine] = outgoing(r)[mine]
-
-    loads[1].wait()
     deep, flat_level = grid_of((depth, layer_count), 0), grid_of((depth, layer_count), 1)
     owner, place = flat_level // lev_local, flat_level % lev_local
     spot = jnp.where(place < half, owner * half + place, LANES + owner * short + place - half)
     ordered = ones_where(deep == spot)
-    lanes = grid_of((depth, LANES), 1)
     zeros = jnp.zeros((depth, LANES - extra), jnp.float32)
 
-    def prepare(s, carry):
-        for g in range(groups):
-            j = g * 8 + s
+    def prepare(t, carry):
+        for h, g in cells:
+            j = g * 8 + h * 4 + t
             turned = f32_dot(ordered, mats_in[j], NT)
             last = jnp.concatenate([turned[:, LANES:], zeros], axis=1)
-            if g:
-                last = pltpu.roll(last, g * part_count * extra, 1)
+            shift = h * half + g * back_step
+            if shift:
+                last = pltpu.roll(last, shift, 1)
             tables[j] = jnp.concatenate([turned[:, :LANES], last], axis=1).astype(jnp.bfloat16)
         return carry
 
-    lax.fori_loop(0, 8, prepare, 0)
-
-    loads[2].wait()
+    lax.fori_loop(0, 4, prepare, 0)
+
+    come, go = grid_of((lev_count * LANES, wide), 0), grid_of((lev_count * LANES, wide), 1)
+    p, lane = come // LANES, come % LANES
+    h, lane = lane // half, lane % half
+    g, lane = lane // fwd_step, lane % fwd_step
+    target = h * LANES + g * rest_step + lane // short * extra + p * short + lane % short
+    spread = ones_where((go == target) & (g < groups))
+
+    loads[1].wait()
     row, col = grid_of((fields, layer_count), 0), grid_of((fields, layer_count), 1)
     chosen = ones_where(col == lev * lev_local + row // part_count)
     coupled_rows = f32_dot(chosen, coupler_in[...], NN)
@@ -185,9 +223,8 @@
     pieces.append(jnp.zeros((2 * fields, LANES - part_count * extra), jnp.float32))
     weights[...] = jnp.concatenate(pieces, axis=1).astype(jnp.bfloat16)
 
-    for copy in loads[3:6]:
+    for copy in loads[2:5]:
         copy.wait()
-    row, col = grid_of((fields, layer_count), 0), grid_of((fields, layer_count), 1)
     gain = jnp.sum(
         jnp.where(col == lev * lev_local + row // part_count, strengths_in[...], 0.0),
         axis=1, keepdims=True,
@@ -204,30 +241,36 @@
 
     lane = grid_of((wave_count, LANES), 1)
     back = []
-    for r in range(row_count):
-        for copy in fwd[r]:
-            copy.wait_recv()
-        for p in range(lev_count):
-            part_in = incoming(r)[pl.ds(p * wave_count, wave_count)].astype(jnp.float32)
-            gathered[p] = part_in[:, :local_n].reshape(block_n, LANES)
-            if r == 0:
-                value = part_in[:, local_n:].reshape(wave_count * 8, LANES)
-                rest_sum = value if p == 0 else rest_sum + value
+
+    def solve_chunk(r):
+        rows_in = by_rows(incoming[r])
+        for q in range(lev_count):
+            main = rows_in[pl.ds(q * wave_count, wave_count), :local_n]
+            gathered[q] = main.astype(jnp.float32).reshape(block_n, LANES)
         if r == 0:
-            rest_in[...] = rest_sum
-
-        def solve(s, carry):
-            rest = rest_in[pl.ds(s, wave_count, stride=8), :]
+            rests = [
+                rows_in[pl.ds(q * wave_count, wave_count), local_n:]
+                .astype(jnp.float32).reshape(wave_count * 4, LANES)
+                for q in range(lev_count)
+            ]
+            value = jnp.concatenate(rests, axis=1).astype(jnp.bfloat16)
+            value = f32_dot(value, spread, NN)
+            for h in range(2):
+                rest_in[h] = value[:, h * LANES:(h + 1) * LANES]
+
+        def solve(t, carry):
+            every = pl.ds(t, wave_count, stride=4)
             lasts = None
-            for g in range(groups):
-                j = g * 8 + s
+            for h, g in cells:
+                j = g * 8 + h * 4 + t
+                rest = rest_in[h, every, :]
                 rows = pl.ds(j, wave_count, stride=local_n)
                 low, high = gathered[0, rows, :], gathered[1, rows, :]
                 sides = [jnp.where(lane < half, low, high),
                          pltpu.roll(jnp.where(lane < half, high, low), half, 1)]
                 stacked = []
                 for c in range(part_count):
-                    shift = g * step + (r * part_count + c) * extra
+                    shift = g * rest_step + (r * part_count + c) * extra
                     moved = pltpu.roll(rest, LANES - shift, 1) if shift else rest
                     stacked.append(jnp.concatenate([sides[c], moved], axis=1)[:, :depth])
                 stacked = jnp.concatenate(stacked, axis=0).astype(jnp.bfloat16)
@@ -239,47 +282,59 @@
             total = lasts[:wave_count]
             for c in range(1, part_count):
                 total += pltpu.roll(lasts[c * wave_count:(c + 1) * wave_count], c * extra, 1)
-            rest_out[pl.ds(s, wave_count, stride=8), :] = total
+            rest_out[every, :] = total
             return carry
 
-        lax.fori_loop(0, 8, solve, 0, unroll=2)
-        pieces = [strided[c].reshape(wave_count, local_n, LANES) for c in range(part_count)]
-        pieces.append(rest_out[...].reshape(wave_count, 8, LANES))
-        back_out[r] = jnp.concatenate(pieces, axis=1).astype(jnp.bfloat16)
-        back.append([])
-        for w, s in wave_peers:
+        lax.fori_loop(0, 4, solve, 0)
+        rows_out = by_rows(back_out)
+        for c in range(part_count):
+            rows_out[r, :, c * local_n:(c + 1) * local_n] = (
+                strided[c].reshape(wave_count, local_n, LANES).astype(jnp.bfloat16)
+            )
+        rows_out[r, :, part_count * local_n:] = (
+            rest_out[...].reshape(wave_count, 4, LANES).astype(jnp.bfloat16)
+        )
+        back.append({})
+        for mask in far_first[:-1]:
             copy = pltpu.make_async_remote_copy(
-                src_ref=back_out.at[r, w], dst_ref=back_in.at[r, wave],
-                send_sem=back_send.at[r, s], recv_sem=back_recv.at[r, s],
-                device_id=(w, lev), device_id_type=MESH,
+                src_ref=back_out.at[r, peer[mask]], dst_ref=back_in.at[r, wave],
+                send_sem=back_send.at[r, mask], recv_sem=back_recv.at[r, mask],
+                device_id=(peer[mask], lev), device_id_type=MESH,
             )
             copy.start()
-            back[r].append(copy)
+            back[r][mask] = copy
         back_in[r, wave] = back_out[r, wave]
 
     relays = [[] for _ in range(row_count)]
-    other = lax.rem(lev + 1, lev_count)
-
-    def relay(r, spot, index):
-        copy = pltpu.make_async_remote_copy(
-            src_ref=back_in.at[r, spot], dst_ref=relayed.at[r, spot],
-            send_sem=relay_send.at[r, index], recv_sem=relay_recv.at[r, index],
-            device_id=(wave, other), device_id_type=MESH,
-        )
-        copy.start()
-        relays[r].append(copy)
+
+    def relay(r, masks):
+        for mask in masks:
+            if mask:
+                back[r][mask].wait_recv()
+            copy = pltpu.make_async_remote_copy(
+                src_ref=(back_in if mask else back_out).at[r, peer[mask]],
+                dst_ref=relayed.at[r, peer[mask]],
+                send_sem=relay_send.at[r, mask], recv_sem=relay_recv.at[r, mask],
+                device_id=(wave, other), device_id_type=MESH,
+            )
+            copy.start()
+            relays[r].append(copy)
 
     heat_flat = heat_in.reshape(row_count, fields, total_n)
     div_flat = div_out.reshape(row_count, fields, total_n)
     temp_flat = temp_out.reshape(row_count, fields, total_n)
 
     def finish(r, wire, block):
-        value = wire[r].astype(jnp.float32)
-        sides = [value[:, c * local_n:(c + 1) * local_n].reshape(block_n, LANES)
-                 for c in range(part_count)]
-        folded = value[:, part_count * local_n:].reshape(wave_count * 8, LANES)
-        turn = part_count * extra
-        rest = [(pltpu.roll(folded, LANES - g * turn, 1) if g else folded)
+        rows_in = by_rows(wire)
+        sides = [
+            rows_in[r, :, c * local_n:(c + 1) * local_n].astype(jnp.float32).reshape(block_n, LANES)
+            for c in range(part_count)
+        ]
+        folded = rows_in[r, :, part_count * local_n:].astype(jnp.float32)
+        swung = pltpu.roll(folded.reshape(wave_count * 4, LANES), half, 1)
+        folded = jnp.concatenate([folded, swung.reshape(wave_count, 4, LANES)], axis=1)
+        folded = folded.reshape(wave_count * 8, LANES)
+        rest = [(pltpu.roll(folded, LANES - g * back_step, 1) if g else folded)
                 .reshape(wave_count, 1, 8, LANES) for g in range(groups)]
         sides.append(jnp.concatenate(rest, axis=1).reshape(block_n, LANES))
         packed = jnp.concatenate(sides, axis=1).astype(jnp.bfloat16)
@@ -291,23 +346,32 @@
         warmed = heat_flat[r, :, spots].astype(jnp.float32) - coupled
         temp_flat[r, :, spots] = jnp.where(inside, warmed, 0.0).astype(jnp.bfloat16)
 
-    loads[6].wait()
+    loads[5].wait()
+    near, mid, far = range(4), range(4, wave_count // 2), range(wave_count // 2, wave_count)
     for r in range(row_count):
-        relay(r, wave, 0)
-        for (w, s), copy in zip(arrivals, back[r]):
+        for copy in fwd[r]:
             copy.wait_recv()
-            relay(r, w, s)
-        finish(r, back_in, lev)
-        if r:
-            for copy in relays[r - 1]:
-                copy.wait_recv()
-            finish(r - 1, relayed, other)
-    for copy in relays[-1]:
+        solve_chunk(r)
+        relay(r, near)
+    for copy in (c for group in fwd for c in group):
+        copy.wait_send()
+    relay(0, mid)
+    relay(0, far)
+    relay(1, mid)
+    finish(0, back_in, lev)
+    relay(1, far)
+    finish(1, back_in, lev)
+    for group in back:
+        for copy in group.values():
+            copy.wait_send()
+    for copy in relays[0]:
+        copy.wait_send()
         copy.wait_recv()
-    finish(row_count - 1, relayed, other)
-    for group in (*fwd, *back, *relays):
-        for copy in group:
-            copy.wait_send()
+    finish(0, relayed, other)
+    for copy in relays[1]:
+        copy.wait_send()
+        copy.wait_recv()
+    finish(1, relayed, other)
 
 
 def store_kernel(*refs):
@@ -335,8 +399,11 @@
     bf16, f32 = jnp.bfloat16, jnp.float32
     field = jax.ShapeDtypeStruct(shape, bf16)
     dma = pltpu.SemaphoreType.DMA
-    back_rows = part_count * local_n + 8
-    wire = pltpu.VMEM((row_count, wave_count, back_rows, LANES), bf16)
+    main_pairs, rest_pairs = local_n // 2, 2
+    wire = pltpu.VMEM((row_count, wave_count, part_count * main_pairs + rest_pairs, 2, LANES), bf16)
+    first = pltpu.VMEM((sources, main_pairs + rest_pairs, 2, LANES), bf16)
+    following = pltpu.VMEM((sources, main_pairs, 2, LANES), bf16)
+    fwd_sems, back_sems = dma((row_count, wave_count, lev_count)), dma((row_count, wave_count))
     outs = pl.pallas_call(
         functools.partial(step_kernel, wave_count, lev_count),
         out_shape=(field,) * 3,
@@ -346,21 +413,16 @@
             pltpu.VMEM(shape, bf16), pltpu.VMEM(shape, bf16), pltpu.VMEM(shape, bf16),
             pltpu.VMEM(matrices.shape[1:], bf16), pltpu.VMEM(coupler.shape, bf16),
             pltpu.VMEM((1, layer_count), f32), pltpu.VMEM((1, row_count), jnp.int32),
-            pltpu.VMEM((sources, local_n + 8, LANES), bf16),
-            pltpu.VMEM((row_count - 1, sources, local_n, LANES), bf16),
-            pltpu.VMEM((sources, local_n + 8, LANES), bf16),
-            pltpu.VMEM((row_count - 1, sources, local_n, LANES), bf16),
+            first, following, first, following,
             pltpu.VMEM((lev_count, block_n, LANES), f32),
-            pltpu.VMEM((wave_count * 8, LANES), f32),
+            pltpu.VMEM((2, wave_count * 4, LANES), f32),
             pltpu.VMEM((local_n, depth, 2 * LANES), bf16),
             pltpu.VMEM((part_count, block_n, LANES), f32),
-            pltpu.VMEM((wave_count * 8, LANES), f32),
+            pltpu.VMEM((wave_count * 4, LANES), f32),
             pltpu.VMEM((2 * fields, 3 * LANES), bf16),
             wire, wire, wire,
-            dma((7,)),
-            dma((row_count, sources)), dma((row_count, sources)),
-            dma((row_count, wave_count)), dma((row_count, wave_count)),
-            dma((row_count, wave_count)), dma((row_count, wave_count)),
+            dma((row_count + 6,)),
+            fwd_sems, fwd_sems, back_sems, back_sems, back_sems, back_sems,
         ],
         compiler_params=pltpu.CompilerParams(
             collective_id=0, has_side_effects=True, vmem_limit_bytes=48 * 2**20
@@ -386,17 +448,22 @@
     row_count, part_count, lev_local, total_n = source_shape
     block_n = total_n // lev_count
     extra = lev_local * lev_count - LANES
+    half = LANES // 2
+    groups = block_n // (8 * wave_count)
     return (
         lev_count == 2
         and part_count == 2
-        and row_count > 1
-        and wave_count > 1
+        and row_count == 2
+        and wave_count > 8
+        and wave_count & (wave_count - 1) == 0
         and wave_count % 8 == 0
         and block_n % LANES == 0
         and total_n % (2 * LANES) == 0
         and block_n % (8 * wave_count) == 0
         and extra > 0
-        and extra * row_count * part_count * (block_n // (8 * wave_count)) <= LANES
+        and extra * row_count * part_count * groups <= LANES
+        and (lev_local - half) * row_count * part_count * groups <= half
+        and extra * part_count * groups <= half
     )
 
 

time: 38.3 us -> 39.4 us (1.029)
  Pallas kernels: 37.5 us -> 38.6 us
    pallas_call x1, Pallas kernels: 36.4 us -> 37.5 us  [by_kernel(): pl.pallas_call(functools.partial(step_kernel, wave_count, lev_count), out...]
where the time goes in v3:
time: 39.4 us; the launch traced here: 39.2 us
  Pallas kernels  38.6 us (98%)
  between operations  0.64 us (2%)
    pallas_call x1, Pallas kernels, by_kernel(): pl.pallas_call(functools.partial(step_kernel, wave_count, lev_count), out...  37.5 us
    pallas_call x1, Pallas kernels, by_kernel(): pl.pallas_call(store_kernel, out_shape=(field,) * 3, in_specs=[vmem] * 3,...  1.06 us

profile of v3, /device:TPU:0, one launch (start us, length us, event | category | flops | bytes accessed | tf_op | source)
XLA Modules:
  0.0 39.2 jit_solution(14526161197959196477)
XLA Ops:
  0.6 37.5 %shard_map.94 = (bf16[2,68,2,768]{3,2,1,0:T(2,128)(2,1)S(1)}, bf16[2,68,2,768]{3,2,1,0:T(2,128)(2,1)S(1)}, bf16[2,68,2,768]{3,2,1,0:T(2,128)(2,1)S(1)}) custom-call(bf16[2,68,2,768]{3,2,1,0:T(2,128)(2,1)} %bitcast.10, bf16[2,68,2,768]{3,2,1,0:T(2,128)(2,1)} %bitcast.11, bf16[2,68,2,768]{3,2,1,0:T(2,128)(2,1)} %bitcast.12, bf16[24,136,136]{2,1,0:T(8,128)(2,1)} %bitcast.9, ...), custom_call_target="tpu_custom_call" | custom-call | tf_op jit(solution)/shard_map/pallas_call | solution.py:407
  38.2 1.1 %shard_map.95 = (bf16[2,68,2,768]{3,2,1,0:T(2,128)(2,1)}, bf16[2,68,2,768]{3,2,1,0:T(2,128)(2,1)}, bf16[2,68,2,768]{3,2,1,0:T(2,128)(2,1)}) custom-call(bf16[2,68,2,768]{3,2,1,0:T(2,128)(2,1)S(1)} %get-tuple-element.9.refs_0_, bf16[2,68,2,768]{3,2,1,0:T(2,128)(2,1)S(1)} %get-tuple-element.10.refs_1_, bf16[2,68,2,768]{3,2,1,0:T(2,128)(2,1)S(1)} %get-tuple-element.11.refs_2_), custom_call_target="tpu_custom_call" | custom-call | tf_op jit(solution)/shard_map/pallas_call | solution.py:439

commit v4 on v3

--- a/solution.py
+++ b/solution.py
@@ -99,18 +99,18 @@
     small = [(matrices, mats_in), (coupler, coupler_in), (strengths, strengths_in),
              (orders, orders_in), (spin, spin_in), (heat, heat_in)]
     for i, (src, dst) in enumerate(
-        [(source.at[r], source_in.at[r]) for r in range(row_count)] + small
+        [(source, source_in), *small]
     ):
         copy = pltpu.make_async_copy(src, dst, load_sem.at[i])
         copy.start()
         loads.append(copy)
-    source_loads, loads = loads[:row_count], loads[row_count:]
+    source_load, loads = loads[0], loads[1:]
 
     peer = [flipped(wave, mask) for mask in range(wave_count)]
     other = lax.rem(lev + 1, lev_count)
-    far_first = range(wave_count - 1, -1, -1)
+    outward = [*range(1, wave_count), 0]
     barrier = pltpu.get_barrier_semaphore()
-    for mask in far_first:
+    for mask in outward:
         for t, q in enumerate((lev, other)):
             if mask or t:
                 pl.semaphore_signal(
@@ -143,26 +143,25 @@
         return ref.reshape(*ref.shape[:-3], ref.shape[-3] * 2, LANES)
 
     outgoing, incoming = [first_out, next_out], [first_in, next_in]
-    fwd = []
+
+    def await_bytes(ref, sem):
+        pltpu.make_async_copy(ref, ref, sem).wait()
 
     def send(r):
-        fwd.append([])
-        for mask in far_first:
+        for mask in outward:
             for t, q in enumerate((lev, other)):
                 if not (mask or t):
                     continue
                 copy = pltpu.make_async_remote_copy(
                     src_ref=outgoing[r].at[q * wave_count + peer[mask]],
                     dst_ref=incoming[r].at[mine],
-                    send_sem=fwd_send.at[r, mask, t], recv_sem=fwd_recv.at[r, mask, t],
+                    send_sem=fwd_send.at[r], recv_sem=fwd_recv.at[r],
                     device_id=(peer[mask], q), device_id_type=MESH,
                 )
                 copy.start()
-                fwd[r].append(copy)
         incoming[r][mine] = outgoing[r][mine]
 
-    for copy in source_loads:
-        copy.wait()
+    source_load.wait()
     main = f32_dot(main_pick, flat[0], NN)
     rest = f32_dot(rest_picks[0], flat[0], NN)
     for r in range(1, row_count):
@@ -240,7 +239,9 @@
         vort_flat[r] = value.astype(jnp.bfloat16)
 
     lane = grid_of((wave_count, LANES), 1)
-    back = []
+    cuts = [1, 4, 8, 12, 16] if wave_count == 16 else [1, 4, 8, wave_count]
+    parties = [range(a, b) for a, b in zip(cuts, cuts[1:])]
+    group_of = {mask: i for i, party in enumerate(parties) for mask in party}
 
     def solve_chunk(r):
         rows_in = by_rows(incoming[r])
@@ -294,31 +295,25 @@
         rows_out[r, :, part_count * local_n:] = (
             rest_out[...].reshape(wave_count, 4, LANES).astype(jnp.bfloat16)
         )
-        back.append({})
-        for mask in far_first[:-1]:
+        for mask in outward[:-1]:
             copy = pltpu.make_async_remote_copy(
                 src_ref=back_out.at[r, peer[mask]], dst_ref=back_in.at[r, wave],
-                send_sem=back_send.at[r, mask], recv_sem=back_recv.at[r, mask],
+                send_sem=back_send.at[r], recv_sem=back_recv.at[r, group_of[mask]],
                 device_id=(peer[mask], lev), device_id_type=MESH,
             )
             copy.start()
-            back[r][mask] = copy
         back_in[r, wave] = back_out[r, wave]
 
-    relays = [[] for _ in range(row_count)]
-
     def relay(r, masks):
+        if masks[0]:
+            await_bytes(back_in.at[r, pl.ds(0, len(masks))], back_recv.at[r, group_of[masks[0]]])
         for mask in masks:
-            if mask:
-                back[r][mask].wait_recv()
-            copy = pltpu.make_async_remote_copy(
+            pltpu.make_async_remote_copy(
                 src_ref=(back_in if mask else back_out).at[r, peer[mask]],
                 dst_ref=relayed.at[r, peer[mask]],
-                send_sem=relay_send.at[r, mask], recv_sem=relay_recv.at[r, mask],
+                send_sem=relay_send.at[r], recv_sem=relay_recv.at[r],
                 device_id=(wave, other), device_id_type=MESH,
-            )
-            copy.start()
-            relays[r].append(copy)
+            ).start()
 
     heat_flat = heat_in.reshape(row_count, fields, total_n)
     div_flat = div_out.reshape(row_count, fields, total_n)
@@ -347,31 +342,29 @@
         temp_flat[r, :, spots] = jnp.where(inside, warmed, 0.0).astype(jnp.bfloat16)
 
     loads[5].wait()
-    near, mid, far = range(4), range(4, wave_count // 2), range(wave_count // 2, wave_count)
     for r in range(row_count):
-        for copy in fwd[r]:
-            copy.wait_recv()
+        await_bytes(incoming[r].at[pl.ds(0, sources - 1)], fwd_recv.at[r])
         solve_chunk(r)
-        relay(r, near)
-    for copy in (c for group in fwd for c in group):
-        copy.wait_send()
-    relay(0, mid)
-    relay(0, far)
-    relay(1, mid)
+        relay(r, [0])
+    lagging, leading = list(parties), list(parties)
+    relay(0, lagging.pop(0))
+    relay(0, lagging.pop(0))
+    while lagging:
+        relay(0, lagging.pop(0))
+        relay(1, leading.pop(0))
+    for r in range(row_count):
+        await_bytes(outgoing[r].at[pl.ds(0, sources - 1)], fwd_send.at[r])
     finish(0, back_in, lev)
-    relay(1, far)
+    while leading:
+        relay(1, leading.pop(0))
     finish(1, back_in, lev)
-    for group in back:
-        for copy in group.values():
-            copy.wait_send()
-    for copy in relays[0]:
-        copy.wait_send()
-        copy.wait_recv()
-    finish(0, relayed, other)
-    for copy in relays[1]:
-        copy.wait_send()
-        copy.wait_recv()
-    finish(1, relayed, other)
+    for r in range(row_count):
+        await_bytes(back_out.at[r, pl.ds(0, wave_count - 1)], back_send.at[r])
+    for r in range(row_count):
+        await_bytes(relayed.at[r], relay_recv.at[r])
+        finish(r, relayed, other)
+    for r in range(row_count):
+        await_bytes(relayed.at[r], relay_send.at[r])
 
 
 def store_kernel(*refs):
@@ -403,7 +396,7 @@
     wire = pltpu.VMEM((row_count, wave_count, part_count * main_pairs + rest_pairs, 2, LANES), bf16)
     first = pltpu.VMEM((sources, main_pairs + rest_pairs, 2, LANES), bf16)
     following = pltpu.VMEM((sources, main_pairs, 2, LANES), bf16)
-    fwd_sems, back_sems = dma((row_count, wave_count, lev_count)), dma((row_count, wave_count))
+    each = dma((row_count,))
     outs = pl.pallas_call(
         functools.partial(step_kernel, wave_count, lev_count),
         out_shape=(field,) * 3,
@@ -421,8 +414,7 @@
             pltpu.VMEM((wave_count * 4, LANES), f32),
             pltpu.VMEM((2 * fields, 3 * LANES), bf16),
             wire, wire, wire,
-            dma((row_count + 6,)),
-            fwd_sems, fwd_sems, back_sems, back_sems, back_sems, back_sems,
+            dma((7,)), each, each, each, dma((row_count, 4)), each, each,
         ],
         compiler_params=pltpu.CompilerParams(
             collective_id=0, has_side_effects=True, vmem_limit_bytes=48 * 2**20

time: 39.4 us -> 34.9 us (0.89)
  Pallas kernels: 38.6 us -> 34.2 us
    pallas_call x1, Pallas kernels: 37.5 us -> 33.1 us  [by_kernel(): pl.pallas_call(functools.partial(step_kernel, wave_count, lev_count), out...]
where the time goes in v4:
time: 34.9 us; the launch traced here: 34.8 us
  Pallas kernels  34.2 us (98%)
  between operations  0.64 us (2%)
    pallas_call x1, Pallas kernels, by_kernel(): pl.pallas_call(functools.partial(step_kernel, wave_count, lev_count), out...  33.1 us
    pallas_call x1, Pallas kernels, by_kernel(): pl.pallas_call(store_kernel, out_shape=(field,) * 3, in_specs=[vmem] * 3,...  1.06 us

profile of v4, /device:TPU:0, one launch (start us, length us, event | category | flops | bytes accessed | tf_op | source)
XLA Modules:
  0.0 34.8 jit_solution(9241157377672864277)
XLA Ops:
  0.6 33.1 %shard_map.94 = (bf16[2,68,2,768]{3,2,1,0:T(2,128)(2,1)S(1)}, bf16[2,68,2,768]{3,2,1,0:T(2,128)(2,1)S(1)}, bf16[2,68,2,768]{3,2,1,0:T(2,128)(2,1)S(1)}) custom-call(bf16[2,68,2,768]{3,2,1,0:T(2,128)(2,1)} %bitcast.10, bf16[2,68,2,768]{3,2,1,0:T(2,128)(2,1)} %bitcast.11, bf16[2,68,2,768]{3,2,1,0:T(2,128)(2,1)} %bitcast.12, bf16[24,136,136]{2,1,0:T(8,128)(2,1)} %bitcast.9, ...), custom_call_target="tpu_custom_call" | custom-call | tf_op jit(solution)/shard_map/pallas_call | solution.py:400
  33.7 1.1 %shard_map.95 = (bf16[2,68,2,768]{3,2,1,0:T(2,128)(2,1)}, bf16[2,68,2,768]{3,2,1,0:T(2,128)(2,1)}, bf16[2,68,2,768]{3,2,1,0:T(2,128)(2,1)}) custom-call(bf16[2,68,2,768]{3,2,1,0:T(2,128)(2,1)S(1)} %get-tuple-element.9.refs_0_, bf16[2,68,2,768]{3,2,1,0:T(2,128)(2,1)S(1)} %get-tuple-element.10.refs_1_, bf16[2,68,2,768]{3,2,1,0:T(2,128)(2,1)S(1)} %get-tuple-element.11.refs_2_), custom_call_target="tpu_custom_call" | custom-call | tf_op jit(solution)/shard_map/pallas_call | solution.py:431

commit v5 on v4

--- a/solution.py
+++ b/solution.py
@@ -106,11 +106,17 @@
         loads.append(copy)
     source_load, loads = loads[0], loads[1:]
 
-    peer = [flipped(wave, mask) for mask in range(wave_count)]
+    middle = wave_count // 2
+    block = lax.rem(wave, 4)
+    across = middle * (1 - lax.div(wave, middle))
+    flips = [flipped(wave, mask) for mask in range(wave_count)]
+    peer = flips[:middle]
+    peer += [across + i // 4 * 4 + flipped(block, i % 4) for i in range(middle)]
+    rank = [*range(middle), *(lax.div(lax.rem(wave, middle), 4) * 4 + i % 4 for i in range(middle))]
     other = lax.rem(lev + 1, lev_count)
     outward = [*range(1, wave_count), 0]
     barrier = pltpu.get_barrier_semaphore()
-    for mask in outward:
+    for mask in reversed(range(wave_count)):
         for t, q in enumerate((lev, other)):
             if mask or t:
                 pl.semaphore_signal(
@@ -147,19 +153,18 @@
     def await_bytes(ref, sem):
         pltpu.make_async_copy(ref, ref, sem).wait()
 
-    def send(r):
-        for mask in outward:
+    def send(r, masks):
+        for mask in masks:
             for t, q in enumerate((lev, other)):
                 if not (mask or t):
                     continue
                 copy = pltpu.make_async_remote_copy(
-                    src_ref=outgoing[r].at[q * wave_count + peer[mask]],
+                    src_ref=outgoing[r].at[q * wave_count + flips[mask]],
                     dst_ref=incoming[r].at[mine],
                     send_sem=fwd_send.at[r], recv_sem=fwd_recv.at[r],
-                    device_id=(peer[mask], q), device_id_type=MESH,
+                    device_id=(flips[mask], q), device_id_type=MESH,
                 )
                 copy.start()
-        incoming[r][mine] = outgoing[r][mine]
 
     source_load.wait()
     main = f32_dot(main_pick, flat[0], NN)
@@ -178,11 +183,13 @@
     )
     by_rows(first_out)[:, local_n:] = folded.astype(jnp.bfloat16)
     pl.semaphore_wait(barrier, sources - 1)
-    send(0)
+    send(0, outward)
+    incoming[0][mine] = outgoing[0][mine]
     for r in range(1, row_count):
         turned = turn(f32_dot(main_pick, flat[r], NN).astype(jnp.bfloat16))
         by_rows(next_out)[...] = turned.reshape(sources, local_n, LANES).astype(jnp.bfloat16)
-        send(r)
+        send(r, range(middle))
+        incoming[r][mine] = outgoing[r][mine]
 
     loads[0].wait()
     deep, flat_level = grid_of((depth, layer_count), 0), grid_of((depth, layer_count), 1)
@@ -238,10 +245,37 @@
         value = jnp.where(n >= orders_in[:, r:r + 1], value, 0.0)
         vort_flat[r] = value.astype(jnp.bfloat16)
 
+    send(1, range(middle, wave_count))
+
     lane = grid_of((wave_count, LANES), 1)
-    cuts = [1, 4, 8, 12, 16] if wave_count == 16 else [1, 4, 8, wave_count]
-    parties = [range(a, b) for a, b in zip(cuts, cuts[1:])]
-    group_of = {mask: i for i, party in enumerate(parties) for mask in party}
+    parties = [range(1, 4), *([i] for i in range(4, wave_count))]
+    group_of = {i: g for g, party in enumerate(parties) for i in party}
+
+    def hand_over(ref, r, spot, target):
+        pltpu.make_async_remote_copy(
+            src_ref=ref, dst_ref=relayed.at[r, spot],
+            send_sem=relay_send.at[r], recv_sem=relay_recv.at[r],
+            device_id=(target, other), device_id_type=MESH,
+        ).start()
+
+    def give_back(r, masks):
+        for mask in masks:
+            copy = pltpu.make_async_remote_copy(
+                src_ref=back_out.at[r, peer[mask]], dst_ref=back_in.at[r, wave],
+                send_sem=back_send.at[r], recv_sem=back_recv.at[
+                    r, group_of[mask] if mask < middle else group_of[middle] + rank[mask]
+                ],
+                device_id=(peer[mask], lev), device_id_type=MESH,
+            )
+            copy.start()
+            if mask in parties[0]:
+                hand_over(back_out.at[r, peer[mask]], r, wave, peer[mask])
+
+    def relay(r, masks):
+        if masks[0]:
+            await_bytes(back_in.at[r, pl.ds(0, len(masks))], back_recv.at[r, group_of[masks[0]]])
+        for mask in masks:
+            hand_over((back_in if mask else back_out).at[r, peer[mask]], r, peer[mask], wave)
 
     def solve_chunk(r):
         rows_in = by_rows(incoming[r])
@@ -286,7 +320,7 @@
             rest_out[every, :] = total
             return carry
 
-        lax.fori_loop(0, 4, solve, 0)
+        lax.fori_loop(0, 4, solve, 0, unroll=4)
         rows_out = by_rows(back_out)
         for c in range(part_count):
             rows_out[r, :, c * local_n:(c + 1) * local_n] = (
@@ -295,25 +329,9 @@
         rows_out[r, :, part_count * local_n:] = (
             rest_out[...].reshape(wave_count, 4, LANES).astype(jnp.bfloat16)
         )
-        for mask in outward[:-1]:
-            copy = pltpu.make_async_remote_copy(
-                src_ref=back_out.at[r, peer[mask]], dst_ref=back_in.at[r, wave],
-                send_sem=back_send.at[r], recv_sem=back_recv.at[r, group_of[mask]],
-                device_id=(peer[mask], lev), device_id_type=MESH,
-            )
-            copy.start()
+        relay(r, [0])
+        give_back(r, range(1, wave_count if r == 0 else middle + 4))
         back_in[r, wave] = back_out[r, wave]
-
-    def relay(r, masks):
-        if masks[0]:
-            await_bytes(back_in.at[r, pl.ds(0, len(masks))], back_recv.at[r, group_of[masks[0]]])
-        for mask in masks:
-            pltpu.make_async_remote_copy(
-                src_ref=(back_in if mask else back_out).at[r, peer[mask]],
-                dst_ref=relayed.at[r, peer[mask]],
-                send_sem=relay_send.at[r], recv_sem=relay_recv.at[r],
-                device_id=(wave, other), device_id_type=MESH,
-            ).start()
 
     heat_flat = heat_in.reshape(row_count, fields, total_n)
     div_flat = div_out.reshape(row_count, fields, total_n)
@@ -345,18 +363,18 @@
     for r in range(row_count):
         await_bytes(incoming[r].at[pl.ds(0, sources - 1)], fwd_recv.at[r])
         solve_chunk(r)
-        relay(r, [0])
-    lagging, leading = list(parties), list(parties)
-    relay(0, lagging.pop(0))
-    relay(0, lagging.pop(0))
-    while lagging:
-        relay(0, lagging.pop(0))
-        relay(1, leading.pop(0))
+    for party in parties[1:]:
+        relay(0, party)
+        place = party[0] - middle
+        if place > 0 and place % 2 and middle + 4 + place // 2 < wave_count:
+            give_back(1, [middle + 4 + place // 2])
     for r in range(row_count):
         await_bytes(outgoing[r].at[pl.ds(0, sources - 1)], fwd_send.at[r])
+    await_bytes(back_in.at[0, pl.ds(0, len(parties[0]))], back_recv.at[0, 0])
     finish(0, back_in, lev)
-    while leading:
-        relay(1, leading.pop(0))
+    for party in parties[1:]:
+        relay(1, party)
+    await_bytes(back_in.at[1, pl.ds(0, len(parties[0]))], back_recv.at[1, 0])
     finish(1, back_in, lev)
     for r in range(row_count):
         await_bytes(back_out.at[r, pl.ds(0, wave_count - 1)], back_send.at[r])
@@ -414,7 +432,7 @@
             pltpu.VMEM((wave_count * 4, LANES), f32),
             pltpu.VMEM((2 * fields, 3 * LANES), bf16),
             wire, wire, wire,
-            dma((7,)), each, each, each, dma((row_count, 4)), each, each,
+            dma((7,)), each, each, each, dma((row_count, wave_count - 3)), each, each,
         ],
         compiler_params=pltpu.CompilerParams(
             collective_id=0, has_side_effects=True, vmem_limit_bytes=48 * 2**20

time: 34.9 us -> 32.8 us (0.940)
  Pallas kernels: 34.2 us -> 32 us
    pallas_call x1, Pallas kernels: 33.1 us -> 31 us  [by_kernel(): pl.pallas_call(functools.partial(step_kernel, wave_count, lev_count), out...]
where the time goes in v5:
time: 32.8 us; the launch traced here: 32.7 us
  Pallas kernels  32 us (98%)
  between operations  0.64 us (2%)
    pallas_call x1, Pallas kernels, by_kernel(): pl.pallas_call(functools.partial(step_kernel, wave_count, lev_count), out...  31 us
    pallas_call x1, Pallas kernels, by_kernel(): pl.pallas_call(store_kernel, out_shape=(field,) * 3, in_specs=[vmem] * 3,...  1.06 us

profile of v5, /device:TPU:0, one launch (start us, length us, event | category | flops | bytes accessed | tf_op | source)
XLA Modules:
  0.0 32.7 jit_solution(11391051969829261545)
XLA Ops:
  0.6 31.0 %shard_map.94 = (bf16[2,68,2,768]{3,2,1,0:T(2,128)(2,1)S(1)}, bf16[2,68,2,768]{3,2,1,0:T(2,128)(2,1)S(1)}, bf16[2,68,2,768]{3,2,1,0:T(2,128)(2,1)S(1)}) custom-call(bf16[2,68,2,768]{3,2,1,0:T(2,128)(2,1)} %bitcast.10, bf16[2,68,2,768]{3,2,1,0:T(2,128)(2,1)} %bitcast.11, bf16[2,68,2,768]{3,2,1,0:T(2,128)(2,1)} %bitcast.12, bf16[24,136,136]{2,1,0:T(8,128)(2,1)} %bitcast.9, ...), custom_call_target="tpu_custom_call" | custom-call | tf_op jit(solution)/shard_map/pallas_call | solution.py:418
  31.6 1.1 %shard_map.95 = (bf16[2,68,2,768]{3,2,1,0:T(2,128)(2,1)}, bf16[2,68,2,768]{3,2,1,0:T(2,128)(2,1)}, bf16[2,68,2,768]{3,2,1,0:T(2,128)(2,1)}) custom-call(bf16[2,68,2,768]{3,2,1,0:T(2,128)(2,1)S(1)} %get-tuple-element.9.refs_0_, bf16[2,68,2,768]{3,2,1,0:T(2,128)(2,1)S(1)} %get-tuple-element.10.refs_1_, bf16[2,68,2,768]{3,2,1,0:T(2,128)(2,1)S(1)} %get-tuple-element.11.refs_2_), custom_call_target="tpu_custom_call" | custom-call | tf_op jit(solution)/shard_map/pallas_call | solution.py:449

commit v6 on v5

--- a/solution.py
+++ b/solution.py
@@ -73,9 +73,9 @@
     wave_count, lev_count, spin, source, heat, matrices, coupler, strengths, orders,
     vort_out, div_out, temp_out,
     spin_in, source_in, heat_in, mats_in, coupler_in, strengths_in, orders_in,
-    first_out, next_out, first_in, next_in, gathered, rest_in, tables, strided, rest_out,
+    first_out, next_out, first_in, next_in, first_lev, next_lev, gathered, rest_in, tables, strided, rest_out,
     weights, back_out, back_in, relayed,
-    load_sem, fwd_send, fwd_recv, back_send, back_recv, relay_send, relay_recv,
+    load_sem, fwd_send, fwd_recv, lev_recv, pass_send, back_send, back_recv, relay_send, relay_recv,
 ):
     wave, lev = lax.axis_index("wave"), lax.axis_index("lev")
     row_count, lev_local, part_count, total_n = source.shape
@@ -153,18 +153,46 @@
     def await_bytes(ref, sem):
         pltpu.make_async_copy(ref, ref, sem).wait()
 
+    crossing = [first_lev, next_lev]
+    home = middle - across
+    planes = [across + i for i in range(0, middle, 4)]
+    planes += [home + lax.rem(lax.rem(wave - block - home, middle) + i, middle)
+               for i in range(4, middle, 4)]
+    planes += [wave - block]
+
+    def cross(r):
+        for i, plane in enumerate(planes):
+            pltpu.make_async_remote_copy(
+                src_ref=outgoing[r].at[pl.ds(other * wave_count + plane, 4)],
+                dst_ref=crossing[r].at[pl.ds(plane, 4)],
+                send_sem=fwd_send.at[r], recv_sem=lev_recv.at[r, i],
+                device_id=(wave, other), device_id_type=MESH,
+            ).start()
+
     def send(r, masks):
         for mask in masks:
-            for t, q in enumerate((lev, other)):
-                if not (mask or t):
-                    continue
-                copy = pltpu.make_async_remote_copy(
-                    src_ref=outgoing[r].at[q * wave_count + flips[mask]],
-                    dst_ref=incoming[r].at[mine],
-                    send_sem=fwd_send.at[r], recv_sem=fwd_recv.at[r],
-                    device_id=(flips[mask], q), device_id_type=MESH,
-                )
-                copy.start()
+            pltpu.make_async_remote_copy(
+                src_ref=outgoing[r].at[lev * wave_count + flips[mask]],
+                dst_ref=incoming[r].at[mine],
+                send_sem=fwd_send.at[r], recv_sem=fwd_recv.at[r],
+                device_id=(flips[mask], lev), device_id_type=MESH,
+            ).start()
+
+    def pass_on(r, which):
+        for i in which:
+            plane = planes[i]
+            await_bytes(crossing[r].at[pl.ds(0, 4)], lev_recv.at[r, i])
+            last = i == len(planes) - 1
+            for k in range(1 if last else 0, 4):
+                target = plane + flipped(block, k)
+                pltpu.make_async_remote_copy(
+                    src_ref=crossing[r].at[target],
+                    dst_ref=incoming[r].at[other * wave_count + wave],
+                    send_sem=pass_send.at[r], recv_sem=fwd_recv.at[r],
+                    device_id=(target, lev), device_id_type=MESH,
+                ).start()
+            if last:
+                incoming[r][other * wave_count + wave] = crossing[r][wave]
 
     source_load.wait()
     main = f32_dot(main_pick, flat[0], NN)
@@ -183,12 +211,13 @@
     )
     by_rows(first_out)[:, local_n:] = folded.astype(jnp.bfloat16)
     pl.semaphore_wait(barrier, sources - 1)
-    send(0, outward)
+    cross(0)
+    send(0, range(1, wave_count))
     incoming[0][mine] = outgoing[0][mine]
     for r in range(1, row_count):
         turned = turn(f32_dot(main_pick, flat[r], NN).astype(jnp.bfloat16))
         by_rows(next_out)[...] = turned.reshape(sources, local_n, LANES).astype(jnp.bfloat16)
-        send(r, range(middle))
+        send(r, range(1, middle))
         incoming[r][mine] = outgoing[r][mine]
 
     loads[0].wait()
@@ -210,6 +239,10 @@
         return carry
 
     lax.fori_loop(0, 4, prepare, 0)
+    cross(1)
+    pass_on(0, range(2))
+    send(1, range(middle, wave_count))
+    pass_on(0, range(2, len(planes)))
 
     come, go = grid_of((lev_count * LANES, wide), 0), grid_of((lev_count * LANES, wide), 1)
     p, lane = come // LANES, come % LANES
@@ -245,8 +278,7 @@
         value = jnp.where(n >= orders_in[:, r:r + 1], value, 0.0)
         vort_flat[r] = value.astype(jnp.bfloat16)
 
-    send(1, range(middle, wave_count))
-
+    pass_on(1, range(len(planes)))
     lane = grid_of((wave_count, LANES), 1)
     parties = [range(1, 4), *([i] for i in range(4, wave_count))]
     group_of = {i: g for g, party in enumerate(parties) for i in party}
@@ -361,7 +393,7 @@
 
     loads[5].wait()
     for r in range(row_count):
-        await_bytes(incoming[r].at[pl.ds(0, sources - 1)], fwd_recv.at[r])
+        await_bytes(incoming[r].at[pl.ds(0, sources - 2)], fwd_recv.at[r])
         solve_chunk(r)
     for party in parties[1:]:
         relay(0, party)
@@ -370,6 +402,7 @@
             give_back(1, [middle + 4 + place // 2])
     for r in range(row_count):
         await_bytes(outgoing[r].at[pl.ds(0, sources - 1)], fwd_send.at[r])
+        await_bytes(crossing[r].at[pl.ds(0, wave_count - 1)], pass_send.at[r])
     await_bytes(back_in.at[0, pl.ds(0, len(parties[0]))], back_recv.at[0, 0])
     finish(0, back_in, lev)
     for party in parties[1:]:
@@ -412,8 +445,13 @@
     dma = pltpu.SemaphoreType.DMA
     main_pairs, rest_pairs = local_n // 2, 2
     wire = pltpu.VMEM((row_count, wave_count, part_count * main_pairs + rest_pairs, 2, LANES), bf16)
-    first = pltpu.VMEM((sources, main_pairs + rest_pairs, 2, LANES), bf16)
-    following = pltpu.VMEM((sources, main_pairs, 2, LANES), bf16)
+
+    def first(count):
+        return pltpu.VMEM((count, main_pairs + rest_pairs, 2, LANES), bf16)
+
+    def following(count):
+        return pltpu.VMEM((count, main_pairs, 2, LANES), bf16)
+
     each = dma((row_count,))
     outs = pl.pallas_call(
         functools.partial(step_kernel, wave_count, lev_count),
@@ -424,7 +462,8 @@
             pltpu.VMEM(shape, bf16), pltpu.VMEM(shape, bf16), pltpu.VMEM(shape, bf16),
             pltpu.VMEM(matrices.shape[1:], bf16), pltpu.VMEM(coupler.shape, bf16),
             pltpu.VMEM((1, layer_count), f32), pltpu.VMEM((1, row_count), jnp.int32),
-            first, following, first, following,
+            first(sources), following(sources), first(sources), following(sources),
+            first(wave_count), following(wave_count),
             pltpu.VMEM((lev_count, block_n, LANES), f32),
             pltpu.VMEM((2, wave_count * 4, LANES), f32),
             pltpu.VMEM((local_n, depth, 2 * LANES), bf16),
@@ -432,7 +471,8 @@
             pltpu.VMEM((wave_count * 4, LANES), f32),
             pltpu.VMEM((2 * fields, 3 * LANES), bf16),
             wire, wire, wire,
-            dma((7,)), each, each, each, dma((row_count, wave_count - 3)), each, each,
+            dma((7,)), each, each, dma((row_count, wave_count // 4)), each,
+            each, dma((row_count, wave_count - 3)), each, each,
         ],
         compiler_params=pltpu.CompilerParams(
             collective_id=0, has_side_effects=True, vmem_limit_bytes=48 * 2**20

time: 32.8 us -> 32.6 us (level)
  no operation moved by 1% of the time
where the time goes in v6:
time: 32.6 us; the launch traced here: 32.4 us
  Pallas kernels  31.8 us (98%)
  between operations  0.64 us (2%)
    pallas_call x1, Pallas kernels, by_kernel(): pl.pallas_call(functools.partial(step_kernel, wave_count, lev_count), out...  30.7 us
    pallas_call x1, Pallas kernels, by_kernel(): pl.pallas_call(store_kernel, out_shape=(field,) * 3, in_specs=[vmem] * 3,...  1.06 us

profile of v6, /device:TPU:0, one launch (start us, length us, event | category | flops | bytes accessed | tf_op | source)
XLA Modules:
  0.0 32.4 jit_solution(17827611096944428857)
XLA Ops:
  0.6 30.7 %shard_map.94 = (bf16[2,68,2,768]{3,2,1,0:T(2,128)(2,1)S(1)}, bf16[2,68,2,768]{3,2,1,0:T(2,128)(2,1)S(1)}, bf16[2,68,2,768]{3,2,1,0:T(2,128)(2,1)S(1)}) custom-call(bf16[2,68,2,768]{3,2,1,0:T(2,128)(2,1)} %bitcast.10, bf16[2,68,2,768]{3,2,1,0:T(2,128)(2,1)} %bitcast.11, bf16[2,68,2,768]{3,2,1,0:T(2,128)(2,1)} %bitcast.12, bf16[24,136,136]{2,1,0:T(8,128)(2,1)} %bitcast.9, ...), custom_call_target="tpu_custom_call" | custom-call | tf_op jit(solution)/shard_map/pallas_call | solution.py:456
  31.4 1.1 %shard_map.95 = (bf16[2,68,2,768]{3,2,1,0:T(2,128)(2,1)}, bf16[2,68,2,768]{3,2,1,0:T(2,128)(2,1)}, bf16[2,68,2,768]{3,2,1,0:T(2,128)(2,1)}) custom-call(bf16[2,68,2,768]{3,2,1,0:T(2,128)(2,1)S(1)} %get-tuple-element.9.refs_0_, bf16[2,68,2,768]{3,2,1,0:T(2,128)(2,1)S(1)} %get-tuple-element.10.refs_1_, bf16[2,68,2,768]{3,2,1,0:T(2,128)(2,1)S(1)} %get-tuple-element.11.refs_2_), custom_call_target="tpu_custom_call" | custom-call | tf_op jit(solution)/shard_map/pallas_call | solution.py:489

commit v7 on v6

--- a/solution.py
+++ b/solution.py
@@ -69,12 +69,46 @@
     return out
 
 
+def by_rows(ref):
+    return ref.reshape(*ref.shape[:-3], ref.shape[-3] * 2, LANES)
+
+
+def block_values(wire, weights, heat_flat, orders, r, block, block_n, step):
+    wave_count = wire.shape[1]
+    local_n = block_n // wave_count
+    groups = local_n // 8
+    fields = heat_flat.shape[1]
+    rows_in = by_rows(wire)
+    parts = (rows_in.shape[2] - 4) // local_n
+    sides = [
+        rows_in[r, :, c * local_n:(c + 1) * local_n].astype(jnp.float32).reshape(block_n, LANES)
+        for c in range(parts)
+    ]
+    folded = rows_in[r, :, parts * local_n:].astype(jnp.float32)
+    swung = pltpu.roll(folded.reshape(wave_count * 4, LANES), LANES // 2, 1)
+    folded = jnp.concatenate([folded, swung.reshape(wave_count, 4, LANES)], axis=1)
+    folded = folded.reshape(wave_count * 8, LANES)
+    rest = [(pltpu.roll(folded, LANES - g * step, 1) if g else folded)
+            .reshape(wave_count, 1, 8, LANES) for g in range(groups)]
+    sides.append(jnp.concatenate(rest, axis=1).reshape(block_n, LANES))
+    packed = jnp.concatenate(sides, axis=1).astype(jnp.bfloat16)
+    result = f32_dot(weights[...], packed, NT)
+    spots = pl.ds(pl.multiple_of(block * block_n, LANES), block_n)
+    inside = block * block_n + grid_of((1, block_n), 1) >= orders[:, r:r + 1]
+    coupled = result[fields:].astype(jnp.bfloat16).astype(jnp.float32)
+    warmed = heat_flat[r, :, spots].astype(jnp.float32) - coupled
+    return (
+        jnp.where(inside, result[:fields], 0.0).astype(jnp.bfloat16),
+        jnp.where(inside, warmed, 0.0).astype(jnp.bfloat16),
+    )
+
+
 def step_kernel(
     wave_count, lev_count, spin, source, heat, matrices, coupler, strengths, orders,
-    vort_out, div_out, temp_out,
-    spin_in, source_in, heat_in, mats_in, coupler_in, strengths_in, orders_in,
+    vort_out, div_out, temp_out, relayed, weights, heat_in, orders_in,
+    spin_in, source_in, mats_in, coupler_in, strengths_in,
     first_out, next_out, first_in, next_in, first_lev, next_lev, gathered, rest_in, tables, strided, rest_out,
-    weights, back_out, back_in, relayed,
+    back_out, back_in,
     load_sem, fwd_send, fwd_recv, lev_recv, pass_send, back_send, back_recv, relay_send, relay_recv,
 ):
     wave, lev = lax.axis_index("wave"), lax.axis_index("lev")
@@ -145,9 +179,6 @@
             [f32_dot(eye, rows[:, k:k + wide], NT) for k in range(0, total_n, wide)], axis=0
         )
 
-    def by_rows(ref):
-        return ref.reshape(*ref.shape[:-3], ref.shape[-3] * 2, LANES)
-
     outgoing, incoming = [first_out, next_out], [first_in, next_in]
 
     def await_bytes(ref, sem):
@@ -241,7 +272,11 @@
     lax.fori_loop(0, 4, prepare, 0)
     cross(1)
     pass_on(0, range(2))
-    send(1, range(middle, wave_count))
+
+    @pl.when(wave >= middle)
+    def _():
+        send(1, range(middle, wave_count))
+
     pass_on(0, range(2, len(planes)))
 
     come, go = grid_of((lev_count * LANES, wide), 0), grid_of((lev_count * LANES, wide), 1)
@@ -277,6 +312,11 @@
         value = (spin_flat[r].astype(jnp.float32) * damping)
         value = jnp.where(n >= orders_in[:, r:r + 1], value, 0.0)
         vort_flat[r] = value.astype(jnp.bfloat16)
+
+
+    @pl.when(wave < middle)
+    def _():
+        send(1, range(middle, wave_count))
 
     pass_on(1, range(len(planes)))
     lane = grid_of((wave_count, LANES), 1)
@@ -362,7 +402,7 @@
             rest_out[...].reshape(wave_count, 4, LANES).astype(jnp.bfloat16)
         )
         relay(r, [0])
-        give_back(r, range(1, wave_count if r == 0 else middle + 4))
+        give_back(r, range(1, wave_count if r == 0 else middle))
         back_in[r, wave] = back_out[r, wave]
 
     heat_flat = heat_in.reshape(row_count, fields, total_n)
@@ -370,36 +410,22 @@
     temp_flat = temp_out.reshape(row_count, fields, total_n)
 
     def finish(r, wire, block):
-        rows_in = by_rows(wire)
-        sides = [
-            rows_in[r, :, c * local_n:(c + 1) * local_n].astype(jnp.float32).reshape(block_n, LANES)
-            for c in range(part_count)
-        ]
-        folded = rows_in[r, :, part_count * local_n:].astype(jnp.float32)
-        swung = pltpu.roll(folded.reshape(wave_count * 4, LANES), half, 1)
-        folded = jnp.concatenate([folded, swung.reshape(wave_count, 4, LANES)], axis=1)
-        folded = folded.reshape(wave_count * 8, LANES)
-        rest = [(pltpu.roll(folded, LANES - g * back_step, 1) if g else folded)
-                .reshape(wave_count, 1, 8, LANES) for g in range(groups)]
-        sides.append(jnp.concatenate(rest, axis=1).reshape(block_n, LANES))
-        packed = jnp.concatenate(sides, axis=1).astype(jnp.bfloat16)
-        result = f32_dot(weights[...], packed, NT)
         spots = pl.ds(pl.multiple_of(block * block_n, LANES), block_n)
-        inside = block * block_n + grid_of((1, block_n), 1) >= orders_in[:, r:r + 1]
-        div_flat[r, :, spots] = jnp.where(inside, result[:fields], 0.0).astype(jnp.bfloat16)
-        coupled = result[fields:].astype(jnp.bfloat16).astype(jnp.float32)
-        warmed = heat_flat[r, :, spots].astype(jnp.float32) - coupled
-        temp_flat[r, :, spots] = jnp.where(inside, warmed, 0.0).astype(jnp.bfloat16)
+        div_flat[r, :, spots], temp_flat[r, :, spots] = block_values(
+            wire, weights, heat_flat, orders_in, r, block, block_n, back_step
+        )
 
     loads[5].wait()
     for r in range(row_count):
         await_bytes(incoming[r].at[pl.ds(0, sources - 2)], fwd_recv.at[r])
         solve_chunk(r)
+    m = middle
+    paced = {4: [m, m + 1], 5: [m + 2, m + 3], 7: [m + 4], m: [m + 5], m + 1: [m + 6],
+             m + 2: range(m + 7, wave_count)}
     for party in parties[1:]:
         relay(0, party)
-        place = party[0] - middle
-        if place > 0 and place % 2 and middle + 4 + place // 2 < wave_count:
-            give_back(1, [middle + 4 + place // 2])
+        if party[0] in paced:
+            give_back(1, paced[party[0]])
     for r in range(row_count):
         await_bytes(outgoing[r].at[pl.ds(0, sources - 1)], fwd_send.at[r])
         await_bytes(crossing[r].at[pl.ds(0, wave_count - 1)], pass_send.at[r])
@@ -413,17 +439,42 @@
         await_bytes(back_out.at[r, pl.ds(0, wave_count - 1)], back_send.at[r])
     for r in range(row_count):
         await_bytes(relayed.at[r], relay_recv.at[r])
-        finish(r, relayed, other)
+        if r + 1 < row_count:
+            finish(r, relayed, other)
     for r in range(row_count):
         await_bytes(relayed.at[r], relay_send.at[r])
 
 
-def store_kernel(*refs):
-    count = (len(refs) - 1) // 2
+def store_kernel(
+    lev_count, step, vort, div, temp, wire, weights, heat, orders, vort_out, div_out, temp_out,
+    div_last, temp_last, sems,
+):
+    row_count, lev_local, part_count, total_n = vort.shape
+    block_n = total_n // lev_count
+    last = row_count - 1
+    lev = lax.axis_index("lev")
+    mine, others = (
+        pl.ds(pl.multiple_of(block * block_n, LANES), block_n)
+        for block in (lev, lax.rem(lev + 1, lev_count))
+    )
+    pairs = [(vort, vort_out)]
+    for src, dst in ((div, div_out), (temp, temp_out)):
+        pairs += [(src.at[r], dst.at[r]) for r in range(last)]
+        pairs.append((src.at[last, :, :, mine], dst.at[last, :, :, mine]))
+    late = [(div_last, div_out.at[last, :, :, others]), (temp_last, temp_out.at[last, :, :, others])]
     copies = [
-        pltpu.make_async_copy(refs[i], refs[count + i], refs[-1].at[i]) for i in range(count)
+        pltpu.make_async_copy(src, dst, sems.at[i]) for i, (src, dst) in enumerate(pairs + late)
     ]
-    for copy in copies:
+    for copy in copies[:len(pairs)]:
+        copy.start()
+    fields = lev_local * part_count
+    values = block_values(
+        wire, weights, heat.reshape(row_count, fields, total_n), orders, last,
+        lax.rem(lev + 1, lev_count), block_n, step,
+    )
+    for ref, value in zip((div_last, temp_last), values):
+        ref.reshape(fields, block_n)[...] = value
+    for copy in copies[len(pairs):]:
         copy.start()
     for copy in copies:
         copy.wait()
@@ -444,7 +495,8 @@
     field = jax.ShapeDtypeStruct(shape, bf16)
     dma = pltpu.SemaphoreType.DMA
     main_pairs, rest_pairs = local_n // 2, 2
-    wire = pltpu.VMEM((row_count, wave_count, part_count * main_pairs + rest_pairs, 2, LANES), bf16)
+    wire_shape = (row_count, wave_count, part_count * main_pairs + rest_pairs, 2, LANES)
+    wire = pltpu.VMEM(wire_shape, bf16)
 
     def first(count):
         return pltpu.VMEM((count, main_pairs + rest_pairs, 2, LANES), bf16)
@@ -455,13 +507,17 @@
     each = dma((row_count,))
     outs = pl.pallas_call(
         functools.partial(step_kernel, wave_count, lev_count),
-        out_shape=(field,) * 3,
+        out_shape=(
+            field, field, field, jax.ShapeDtypeStruct(wire_shape, bf16),
+            jax.ShapeDtypeStruct((2 * fields, 3 * LANES), bf16), field,
+            jax.ShapeDtypeStruct((1, row_count), jnp.int32),
+        ),
         in_specs=[anywhere] * 7,
-        out_specs=(vmem,) * 3,
+        out_specs=(vmem,) * 7,
         scratch_shapes=[
-            pltpu.VMEM(shape, bf16), pltpu.VMEM(shape, bf16), pltpu.VMEM(shape, bf16),
+            pltpu.VMEM(shape, bf16), pltpu.VMEM(shape, bf16),
             pltpu.VMEM(matrices.shape[1:], bf16), pltpu.VMEM(coupler.shape, bf16),
-            pltpu.VMEM((1, layer_count), f32), pltpu.VMEM((1, row_count), jnp.int32),
+            pltpu.VMEM((1, layer_count), f32),
             first(sources), following(sources), first(sources), following(sources),
             first(wave_count), following(wave_count),
             pltpu.VMEM((lev_count, block_n, LANES), f32),
@@ -469,8 +525,7 @@
             pltpu.VMEM((local_n, depth, 2 * LANES), bf16),
             pltpu.VMEM((part_count, block_n, LANES), f32),
             pltpu.VMEM((wave_count * 4, LANES), f32),
-            pltpu.VMEM((2 * fields, 3 * LANES), bf16),
-            wire, wire, wire,
+            wire, wire,
             dma((7,)), each, each, dma((row_count, wave_count // 4)), each,
             each, dma((row_count, wave_count - 3)), each, each,
         ],
@@ -486,10 +541,13 @@
             )
         )
     )
+    extra = layer_count - LANES
+    last_block = pltpu.VMEM((lev_local, part_count, block_n), bf16)
     outs = pl.pallas_call(
-        store_kernel, out_shape=(field,) * 3, in_specs=[vmem] * 3, out_specs=(anywhere,) * 3,
-        scratch_shapes=[dma((3,))],
-        compiler_params=pltpu.CompilerParams(vmem_limit_bytes=4 * 2**20),
+        functools.partial(store_kernel, lev_count, part_count * extra),
+        out_shape=(field,) * 3, in_specs=[vmem] * 7, out_specs=(anywhere,) * 3,
+        scratch_shapes=[last_block, last_block, dma((2 * row_count + 3,))],
+        compiler_params=pltpu.CompilerParams(vmem_limit_bytes=8 * 2**20),
     )(*outs)
     return tuple(out.transpose(0, 2, 1, 3) for out in outs)
 

time: 32.6 us -> 31.7 us (0.972)
  Pallas kernels: 31.8 us -> 30.9 us
    pallas_call x1, Pallas kernels: 30.7 us -> 29.7 us  [by_kernel(): pl.pallas_call(functools.partial(step_kernel, wave_count, lev_count), out...]
where the time goes in v7:
time: 31.7 us; the launch traced here: 31.5 us
  Pallas kernels  30.9 us (97%)
  between operations  0.64 us (2%)
    pallas_call x1, Pallas kernels, by_kernel(): pl.pallas_call(functools.partial(step_kernel, wave_count, lev_count), out...  29.7 us
    pallas_call x1, Pallas kernels, by_kernel(): pl.pallas_call(functools.partial(store_kernel, lev_count, part_count * ex...  1.21 us

profile of v7, /device:TPU:0, one launch (start us, length us, event | category | flops | bytes accessed | tf_op | source)
XLA Modules:
  0.0 31.5 jit_solution(7308390327154076274)
XLA Ops:
  0.6 29.7 %shard_map.94 = (bf16[2,68,2,768]{3,2,1,0:T(2,128)(2,1)S(1)}, bf16[2,68,2,768]{3,2,1,0:T(2,128)(2,1)S(1)}, bf16[2,68,2,768]{3,2,1,0:T(2,128)(2,1)S(1)}, bf16[2,1...) custom-call(bf16[2,68,2,768]{3,2,1,0:T(2,128)(2,1)} %bitcast.10, ...), custom_call_target="tpu_custom_call" | custom-call | tf_op jit(solution)/shard_map/pallas_call | solution.py:508
  30.3 1.2 %shard_map.95 = (bf16[2,68,2,768]{3,2,1,0:T(2,128)(2,1)}, bf16[2,68,2,768]{3,2,1,0:T(2,128)(2,1)}, bf16[2,68,2,768]{3,2,1,0:T(2,128)(2,1)}) custom-call(bf16[2,68,2,768]{3,2,1,0:T(2,128)(2,1)S(1)} %get-tuple-element.13.vort, bf16[2,68,2,768]{3,2,1,0:T(2,128)(2,1)S(1)} %get-tuple-element.14.div, bf16[2,68,2,768]{3,2,1,0:T(2,128)(2,1)S(1)} %get-tuple-element.15.temp, ...), custom_call_target="tpu_custom_call" | custom-call | tf_op jit(solution)/shard_map/pallas_call | solution.py:546

commit v8 on v7

--- a/solution.py
+++ b/solution.py
@@ -129,6 +129,26 @@
     back_step = part_count * extra
     rest_step = row_count * part_count * extra
 
+    middle = wave_count // 2
+    block = lax.rem(wave, 4)
+    across = middle * (1 - lax.div(wave, middle))
+    flips = [flipped(wave, mask) for mask in range(wave_count)]
+    peer = flips[:middle]
+    peer += [across + i // 4 * 4 + flipped(block, i % 4) for i in range(middle)]
+    rank = [*range(middle), *(lax.div(lax.rem(wave, middle), 4) * 4 + i % 4 for i in range(middle))]
+    other = lax.rem(lev + 1, lev_count)
+    outward = [*range(1, wave_count), 0]
+    barrier = pltpu.get_barrier_semaphore()
+
+    def greet(masks):
+        for mask in masks:
+            for t, q in enumerate((lev, other)):
+                if mask or t:
+                    pl.semaphore_signal(
+                        barrier, inc=1, device_id=(flips[mask], q), device_id_type=MESH
+                    )
+
+    greet(range(wave_count - 1, middle - 1, -1))
     loads = []
     small = [(matrices, mats_in), (coupler, coupler_in), (strengths, strengths_in),
              (orders, orders_in), (spin, spin_in), (heat, heat_in)]
@@ -140,22 +160,7 @@
         loads.append(copy)
     source_load, loads = loads[0], loads[1:]
 
-    middle = wave_count // 2
-    block = lax.rem(wave, 4)
-    across = middle * (1 - lax.div(wave, middle))
-    flips = [flipped(wave, mask) for mask in range(wave_count)]
-    peer = flips[:middle]
-    peer += [across + i // 4 * 4 + flipped(block, i % 4) for i in range(middle)]
-    rank = [*range(middle), *(lax.div(lax.rem(wave, middle), 4) * 4 + i % 4 for i in range(middle))]
-    other = lax.rem(lev + 1, lev_count)
-    outward = [*range(1, wave_count), 0]
-    barrier = pltpu.get_barrier_semaphore()
-    for mask in reversed(range(wave_count)):
-        for t, q in enumerate((lev, other)):
-            if mask or t:
-                pl.semaphore_signal(
-                    barrier, inc=1, device_id=(peer[mask], q), device_id_type=MESH
-                )
+    greet(range(middle - 1, -1, -1))
 
     out_row, in_row = grid_of((wide, fields), 0), grid_of((wide, fields), 1)
     level, part = in_row // part_count, in_row % part_count
@@ -320,8 +325,12 @@
 
     pass_on(1, range(len(planes)))
     lane = grid_of((wave_count, LANES), 1)
-    parties = [range(1, 4), *([i] for i in range(4, wave_count))]
-    group_of = {i: g for g, party in enumerate(parties) for i in party}
+    near, mid, widths = range(1, 4), range(4, middle), (2, 1)
+    parties = [
+        [near, mid, *(range(i, i + width) for i in range(middle, wave_count, width))]
+        for width in widths
+    ]
+    first_group = (0, len(parties[0]))
 
     def hand_over(ref, r, spot, target):
         pltpu.make_async_remote_copy(
@@ -335,17 +344,23 @@
             copy = pltpu.make_async_remote_copy(
                 src_ref=back_out.at[r, peer[mask]], dst_ref=back_in.at[r, wave],
                 send_sem=back_send.at[r], recv_sem=back_recv.at[
-                    r, group_of[mask] if mask < middle else group_of[middle] + rank[mask]
+                    first_group[r] + (
+                        (mask >= 4) if mask < middle else 2 + lax.div(rank[mask], widths[r])
+                    )
                 ],
                 device_id=(peer[mask], lev), device_id_type=MESH,
             )
             copy.start()
-            if mask in parties[0]:
+            if mask in near:
                 hand_over(back_out.at[r, peer[mask]], r, wave, peer[mask])
+
+    def await_group(r, group):
+        party = parties[r][group]
+        await_bytes(back_in.at[r, pl.ds(0, len(party))], back_recv.at[first_group[r] + group])
 
     def relay(r, masks):
         if masks[0]:
-            await_bytes(back_in.at[r, pl.ds(0, len(masks))], back_recv.at[r, group_of[masks[0]]])
+            await_group(r, parties[r].index(masks))
         for mask in masks:
             hand_over((back_in if mask else back_out).at[r, peer[mask]], r, peer[mask], wave)
 
@@ -402,7 +417,7 @@
             rest_out[...].reshape(wave_count, 4, LANES).astype(jnp.bfloat16)
         )
         relay(r, [0])
-        give_back(r, range(1, wave_count if r == 0 else middle))
+        give_back(r, range(1, wave_count if r == 0 else middle + 4))
         back_in[r, wave] = back_out[r, wave]
 
     heat_flat = heat_in.reshape(row_count, fields, total_n)
@@ -419,21 +434,30 @@
     for r in range(row_count):
         await_bytes(incoming[r].at[pl.ds(0, sources - 2)], fwd_recv.at[r])
         solve_chunk(r)
-    m = middle
-    paced = {4: [m, m + 1], 5: [m + 2, m + 3], 7: [m + 4], m: [m + 5], m + 1: [m + 6],
-             m + 2: range(m + 7, wave_count)}
-    for party in parties[1:]:
+    def on_half(high, r):
+        @pl.when((wave >= middle) if high else (wave < middle))
+        def _():
+            relay(r, mid)
+
+    on_half(True, 0)
+    give_back(1, [middle + 4])
+    for i, party in enumerate(parties[0][2:]):
         relay(0, party)
-        if party[0] in paced:
-            give_back(1, paced[party[0]])
+        if i == 0:
+            give_back(1, [middle + 5])
+        if i == 1:
+            give_back(1, range(middle + 6, wave_count))
+            on_half(False, 0)
+            on_half(True, 1)
+    on_half(False, 1)
     for r in range(row_count):
         await_bytes(outgoing[r].at[pl.ds(0, sources - 1)], fwd_send.at[r])
         await_bytes(crossing[r].at[pl.ds(0, wave_count - 1)], pass_send.at[r])
-    await_bytes(back_in.at[0, pl.ds(0, len(parties[0]))], back_recv.at[0, 0])
+    await_group(0, 0)
     finish(0, back_in, lev)
-    for party in parties[1:]:
+    for party in parties[1][2:]:
         relay(1, party)
-    await_bytes(back_in.at[1, pl.ds(0, len(parties[0]))], back_recv.at[1, 0])
+    await_group(1, 0)
     finish(1, back_in, lev)
     for r in range(row_count):
         await_bytes(back_out.at[r, pl.ds(0, wave_count - 1)], back_send.at[r])
@@ -527,7 +551,7 @@
             pltpu.VMEM((wave_count * 4, LANES), f32),
             wire, wire,
             dma((7,)), each, each, dma((row_count, wave_count // 4)), each,
-            each, dma((row_count, wave_count - 3)), each, each,
+            each, dma((4 + wave_count // 4 + wave_count // 2,)), each, each,
         ],
         compiler_params=pltpu.CompilerParams(
             collective_id=0, has_side_effects=True, vmem_limit_bytes=48 * 2**20

time: 31.7 us -> 31.4 us (level)
  no operation moved by 1% of the time
where the time goes in v8:
time: 31.4 us; the launch traced here: 31.3 us
  Pallas kernels  30.6 us (97%)
  between operations  0.64 us (2%)
    pallas_call x1, Pallas kernels, by_kernel(): pl.pallas_call(functools.partial(step_kernel, wave_count, lev_count), out...  29.4 us
    pallas_call x1, Pallas kernels, by_kernel(): pl.pallas_call(functools.partial(store_kernel, lev_count, part_count * ex...  1.21 us

profile of v8, /device:TPU:0, one launch (start us, length us, event | category | flops | bytes accessed | tf_op | source)
XLA Modules:
  0.0 31.3 jit_solution(14356377377936977622)
XLA Ops:
  0.6 29.4 %shard_map.94 = (bf16[2,68,2,768]{3,2,1,0:T(2,128)(2,1)S(1)}, bf16[2,68,2,768]{3,2,1,0:T(2,128)(2,1)S(1)}, bf16[2,68,2,768]{3,2,1,0:T(2,128)(2,1)S(1)}, bf16[2,1...) custom-call(bf16[2,68,2,768]{3,2,1,0:T(2,128)(2,1)} %bitcast.10, ...), custom_call_target="tpu_custom_call" | custom-call | tf_op jit(solution)/shard_map/pallas_call | solution.py:532
  30.1 1.2 %shard_map.95 = (bf16[2,68,2,768]{3,2,1,0:T(2,128)(2,1)}, bf16[2,68,2,768]{3,2,1,0:T(2,128)(2,1)}, bf16[2,68,2,768]{3,2,1,0:T(2,128)(2,1)}) custom-call(bf16[2,68,2,768]{3,2,1,0:T(2,128)(2,1)S(1)} %get-tuple-element.13.vort, bf16[2,68,2,768]{3,2,1,0:T(2,128)(2,1)S(1)} %get-tuple-element.14.div, bf16[2,68,2,768]{3,2,1,0:T(2,128)(2,1)S(1)} %get-tuple-element.15.temp, ...), custom_call_target="tpu_custom_call" | custom-call | tf_op jit(solution)/shard_map/pallas_call | solution.py:570

commit v9 on v8

--- a/solution.py
+++ b/solution.py
@@ -434,12 +434,12 @@
     for r in range(row_count):
         await_bytes(incoming[r].at[pl.ds(0, sources - 2)], fwd_recv.at[r])
         solve_chunk(r)
-    def on_half(high, r):
-        @pl.when((wave >= middle) if high else (wave < middle))
+    def mid_if(condition, r):
+        @pl.when(condition)
         def _():
             relay(r, mid)
 
-    on_half(True, 0)
+    mid_if(wave >= 4, 0)
     give_back(1, [middle + 4])
     for i, party in enumerate(parties[0][2:]):
         relay(0, party)
@@ -447,9 +447,10 @@
             give_back(1, [middle + 5])
         if i == 1:
             give_back(1, range(middle + 6, wave_count))
-            on_half(False, 0)
-            on_half(True, 1)
-    on_half(False, 1)
+            mid_if(wave >= middle, 1)
+        if i == 2:
+            mid_if(wave < 4, 0)
+    mid_if(wave < middle, 1)
     for r in range(row_count):
         await_bytes(outgoing[r].at[pl.ds(0, sources - 1)], fwd_send.at[r])
         await_bytes(crossing[r].at[pl.ds(0, wave_count - 1)], pass_send.at[r])

time: 31.4 us -> 30.9 us (0.984)
  Pallas kernels: 30.6 us -> 30.1 us
    pallas_call x1, Pallas kernels: 29.4 us -> 28.9 us  [by_kernel(): pl.pallas_call(functools.partial(step_kernel, wave_count, lev_count), out...]
where the time goes in v9:
time: 30.9 us; the launch traced here: 30.7 us
  Pallas kernels  30.1 us (97%)
  between operations  0.64 us (2%)
    pallas_call x1, Pallas kernels, by_kernel(): pl.pallas_call(functools.partial(step_kernel, wave_count, lev_count), out...  28.9 us
    pallas_call x1, Pallas kernels, by_kernel(): pl.pallas_call(functools.partial(store_kernel, lev_count, part_count * ex...  1.21 us

profile of v9, /device:TPU:0, one launch (start us, length us, event | category | flops | bytes accessed | tf_op | source)
XLA Modules:
  0.0 30.7 jit_solution(7321355499750349138)
XLA Ops:
  0.6 28.9 %shard_map.94 = (bf16[2,68,2,768]{3,2,1,0:T(2,128)(2,1)S(1)}, bf16[2,68,2,768]{3,2,1,0:T(2,128)(2,1)S(1)}, bf16[2,68,2,768]{3,2,1,0:T(2,128)(2,1)S(1)}, bf16[2,1...) custom-call(bf16[2,68,2,768]{3,2,1,0:T(2,128)(2,1)} %bitcast.10, ...), custom_call_target="tpu_custom_call" | custom-call | tf_op jit(solution)/shard_map/pallas_call | solution.py:533
  29.5 1.2 %shard_map.95 = (bf16[2,68,2,768]{3,2,1,0:T(2,128)(2,1)}, bf16[2,68,2,768]{3,2,1,0:T(2,128)(2,1)}, bf16[2,68,2,768]{3,2,1,0:T(2,128)(2,1)}) custom-call(bf16[2,68,2,768]{3,2,1,0:T(2,128)(2,1)S(1)} %get-tuple-element.13.vort, bf16[2,68,2,768]{3,2,1,0:T(2,128)(2,1)S(1)} %get-tuple-element.14.div, bf16[2,68,2,768]{3,2,1,0:T(2,128)(2,1)S(1)} %get-tuple-element.15.temp, ...), custom_call_target="tpu_custom_call" | custom-call | tf_op jit(solution)/shard_map/pallas_call | solution.py:571

commit v10 on v9

--- a/solution.py
+++ b/solution.py
@@ -134,8 +134,12 @@
     across = middle * (1 - lax.div(wave, middle))
     flips = [flipped(wave, mask) for mask in range(wave_count)]
     peer = flips[:middle]
-    peer += [across + i // 4 * 4 + flipped(block, i % 4) for i in range(middle)]
-    rank = [*range(middle), *(lax.div(lax.rem(wave, middle), 4) * 4 + i % 4 for i in range(middle))]
+    side, core = lax.div(block, 2), lax.rem(block, 2)
+    peer += [across + i // 2 * 2 + flipped(core, i % 2) for i in range(middle)]
+    rank = [
+        lax.div(lax.rem(wave, middle), 4) * 4 + side * 2 + i % 2 for i in range(middle)
+    ]
+    rank = [*range(middle), *rank]
     other = lax.rem(lev + 1, lev_count)
     outward = [*range(1, wave_count), 0]
     barrier = pltpu.get_barrier_semaphore()

time: 30.9 us -> 30.8 us (level)
  no operation moved by 1% of the time
where the time goes in v10:
time: 30.8 us; the launch traced here: 30.6 us
  Pallas kernels  30 us (97%)
  between operations  0.64 us (2%)
    pallas_call x1, Pallas kernels, by_kernel(): pl.pallas_call(functools.partial(step_kernel, wave_count, lev_count), out...  28.8 us
    pallas_call x1, Pallas kernels, by_kernel(): pl.pallas_call(functools.partial(store_kernel, lev_count, part_count * ex...  1.21 us

profile of v10, /device:TPU:0, one launch (start us, length us, event | category | flops | bytes accessed | tf_op | source)
XLA Modules:
  0.0 30.6 jit_solution(13193937073313045379)
XLA Ops:
  0.6 28.8 %shard_map.94 = (bf16[2,68,2,768]{3,2,1,0:T(2,128)(2,1)S(1)}, bf16[2,68,2,768]{3,2,1,0:T(2,128)(2,1)S(1)}, bf16[2,68,2,768]{3,2,1,0:T(2,128)(2,1)S(1)}, bf16[2,1...) custom-call(bf16[2,68,2,768]{3,2,1,0:T(2,128)(2,1)} %bitcast.10, ...), custom_call_target="tpu_custom_call" | custom-call | tf_op jit(solution)/shard_map/pallas_call | solution.py:537
  29.4 1.2 %shard_map.95 = (bf16[2,68,2,768]{3,2,1,0:T(2,128)(2,1)}, bf16[2,68,2,768]{3,2,1,0:T(2,128)(2,1)}, bf16[2,68,2,768]{3,2,1,0:T(2,128)(2,1)}) custom-call(bf16[2,68,2,768]{3,2,1,0:T(2,128)(2,1)S(1)} %get-tuple-element.13.vort, bf16[2,68,2,768]{3,2,1,0:T(2,128)(2,1)S(1)} %get-tuple-element.14.div, bf16[2,68,2,768]{3,2,1,0:T(2,128)(2,1)S(1)} %get-tuple-element.15.temp, ...), custom_call_target="tpu_custom_call" | custom-call | tf_op jit(solution)/shard_map/pallas_call | solution.py:575

commit v11 on v10

--- a/solution.py
+++ b/solution.py
@@ -458,10 +458,10 @@
     for r in range(row_count):
         await_bytes(outgoing[r].at[pl.ds(0, sources - 1)], fwd_send.at[r])
         await_bytes(crossing[r].at[pl.ds(0, wave_count - 1)], pass_send.at[r])
+    for party in parties[1][2:]:
+        relay(1, party)
     await_group(0, 0)
     finish(0, back_in, lev)
-    for party in parties[1][2:]:
-        relay(1, party)
     await_group(1, 0)
     finish(1, back_in, lev)
     for r in range(row_count):

time: 30.8 us -> 30.8 us (level)
  no operation moved by 1% of the time
where the time goes in v11:
time: 30.8 us; the launch traced here: 30.6 us
  Pallas kernels  30 us (97%)
  between operations  0.64 us (2%)
    pallas_call x1, Pallas kernels, by_kernel(): pl.pallas_call(functools.partial(step_kernel, wave_count, lev_count), out...  28.8 us
    pallas_call x1, Pallas kernels, by_kernel(): pl.pallas_call(functools.partial(store_kernel, lev_count, part_count * ex...  1.21 us

profile of v11, /device:TPU:0, one launch (start us, length us, event | category | flops | bytes accessed | tf_op | source)
XLA Modules:
  0.0 30.6 jit_solution(6835576480607515834)
XLA Ops:
  0.6 28.8 %shard_map.94 = (bf16[2,68,2,768]{3,2,1,0:T(2,128)(2,1)S(1)}, bf16[2,68,2,768]{3,2,1,0:T(2,128)(2,1)S(1)}, bf16[2,68,2,768]{3,2,1,0:T(2,128)(2,1)S(1)}, bf16[2,1...) custom-call(bf16[2,68,2,768]{3,2,1,0:T(2,128)(2,1)} %bitcast.10, ...), custom_call_target="tpu_custom_call" | custom-call | tf_op jit(solution)/shard_map/pallas_call | solution.py:537
  29.4 1.2 %shard_map.95 = (bf16[2,68,2,768]{3,2,1,0:T(2,128)(2,1)}, bf16[2,68,2,768]{3,2,1,0:T(2,128)(2,1)}, bf16[2,68,2,768]{3,2,1,0:T(2,128)(2,1)}) custom-call(bf16[2,68,2,768]{3,2,1,0:T(2,128)(2,1)S(1)} %get-tuple-element.13.vort, bf16[2,68,2,768]{3,2,1,0:T(2,128)(2,1)S(1)} %get-tuple-element.14.div, bf16[2,68,2,768]{3,2,1,0:T(2,128)(2,1)S(1)} %get-tuple-element.15.temp, ...), custom_call_target="tpu_custom_call" | custom-call | tf_op jit(solution)/shard_map/pallas_call | solution.py:575
